TPU v7x, 32 devices: a whole 2x2x4 slice. The times are simulated.
32 devices in a mesh: dp: 4 (over x, core), ctx: 8 (over z, y).
Axes of the slice: x: 2, y: 2, z: 4, core: 2. Of those that a mesh axis runs over, the one named last changes fastest.
Arguments:
- grad_output: bfloat16 [4, 2048, 1024], P('dp', None, 'ctx'), may hold values from -6 to 6
- post_gate: bfloat16 [4, 2048, 1024], P('dp', None, 'ctx'), may hold values from -6 to 6
- pre_gate: bfloat16 [4, 2048, 1024], P('dp', None, 'ctx'), may hold values from -6 to 6
- value_branch: bfloat16 [4, 2048, 1024], P('dp', None, 'ctx'), may hold values from -6 to 6
- long_filter: float32 [2048, 1024], P('ctx'), may hold values from -0.1875 to 0.1875
- skip_weight: float32 [2048], replicated, may hold values from -3 to 3
Outputs:
- grad_pre_gate: bfloat16 [4, 2048, 1024], P('dp', None, 'ctx')
- grad_value_branch: bfloat16 [4, 2048, 1024], P('dp', None, 'ctx')
- grad_long_filter: float32 [2048, 1024], P('ctx', 'dp')
All inputs are finite; a program needn't handle non-finite values.
Results may differ from a plain program's by a relative error of at most 0.0095.
Values may be sent and summed in bfloat16 or wider, within the bound.
No kernel may reach another device: no remote copies, remote signals or barrier semaphores. Data moves between devices by JAX's collectives and lax.ppermute only.
A program may use at most 64 MiB of HBM per device.

v0:
```python
import functools
import math

import jax
import jax.numpy as jnp
import numpy as np
from jax import lax
from jax.experimental import pallas as pl
from jax.experimental.pallas import tpu as pltpu
from jax.sharding import PartitionSpec as P


highest = lax.Precision.HIGHEST
f32 = jnp.float32
bf16 = jnp.bfloat16
LANES = 128
VMEM_MIB = 12


def half_matrix(length):
    time = np.arange(length // 2)[:, None]
    phase = (time * np.arange(length)[None, :] % (2 * length)) * (math.pi / length)
    pair = np.stack([np.cos(phase), -np.sin(phase)], axis=1)
    pair[:, 1, 0] = 1.0 - 2.0 * (time[:, 0] % 2)
    tiles = pair.reshape(length // 2, 2, length // LANES, LANES).transpose(0, 2, 1, 3)
    return jnp.asarray(tiles.reshape(length // 2, 2 * length), bf16)


def in_hbm(*arrays):
    return [pltpu.with_memory_space_constraint(array, pltpu.HBM) for array in arrays]


def peer_rows(axis, k, rows):
    return pl.ds(pl.multiple_of((lax.axis_index(axis) ^ k) * rows, rows), rows)


def call(kernel, out_specs, out_shape, scratch, flops, moved, mib, operands, in_specs=None):
    vmem = pl.BlockSpec(memory_space=pltpu.VMEM)
    return list(pl.pallas_call(
        kernel,
        in_specs=in_specs or [vmem] * len(operands),
        out_specs=out_specs or [vmem] * len(out_shape),
        out_shape=out_shape,
        scratch_shapes=scratch,
        compiler_params=pltpu.CompilerParams(vmem_limit_bytes=mib * 2**20),
        cost_estimate=pl.CostEstimate(flops=flops, bytes_accessed=moved, transcendentals=0),
    )(*operands))


def product_kernel(axis, near, far, *refs):
    in_refs, out_refs = refs[:4], refs[4:-2]
    buf_ref, sems = refs[-2:]
    both_refs = dict(zip(near, out_refs))
    gated_refs = dict(zip(far, out_refs[len(near) :]))
    saved_refs = dict(zip(far, out_refs[len(near) + len(far) :]))
    rows = buf_ref.shape[2]
    copies = {}
    for k in far + near:
        copies[k] = [
            pltpu.make_async_copy(
                in_ref.at[peer_rows(axis, k, rows)], buf_ref.at[j, k], sems.at[j, k]
            )
            for j, in_ref in enumerate(in_refs)
        ]
        for copy in copies[k]:
            copy.start()
    for k in far + near:
        for copy in copies[k]:
            copy.wait()
        gated = (buf_ref[0, k].astype(f32) * buf_ref[1, k].astype(f32)).astype(bf16)
        saved = (buf_ref[2, k].astype(f32) * buf_ref[3, k].astype(f32)).astype(bf16)
        if k in both_refs:
            both_refs[k][0] = gated
            both_refs[k][1] = saved
        else:
            gated_refs[k][...] = gated
            saved_refs[k][...] = saved


def product(arrays, near, far, axis):
    count = len(near) + len(far)
    channels, block = arrays[0].shape
    rows = channels // count
    out = call(
        functools.partial(product_kernel, axis, near, far),
        None,
        [jax.ShapeDtypeStruct((2, rows, block), bf16)] * len(near)
        + [jax.ShapeDtypeStruct((rows, block), bf16)] * (2 * len(far)),
        [pltpu.VMEM((4, count, rows, block), bf16), pltpu.SemaphoreType.DMA((4, count))],
        2 * channels * block,
        12 * channels * block,
        4,
        in_hbm(*arrays),
        [pl.BlockSpec(memory_space=pltpu.HBM)] * 4,
    )
    ends = [len(near), count, count + len(far)]
    return [dict(zip(ks, out[lo:hi])) for ks, lo, hi in zip((near, far, far), [0] + ends, ends)]


def filter_kernel(filt_ref, low_ref, high_ref, spec_ref):
    length = filt_ref.shape[1]
    half = length // 2
    filt = filt_ref[...].astype(bf16)
    turn = lax.broadcasted_iota(jnp.int32, (1, LANES), 1) % 4
    keep = jnp.where(turn == 0, 1.0, jnp.where(turn == 2, -1.0, 0.0)).astype(bf16)
    swap = jnp.where(turn == 1, 1.0, jnp.where(turn == 3, -1.0, 0.0)).astype(bf16)
    for n in range(length // LANES):
        re = pl.ds(2 * n * LANES, LANES)
        im = pl.ds((2 * n + 1) * LANES, LANES)
        both = pl.ds(2 * n * LANES, 2 * LANES)
        cosine = low_ref[:, re]
        minus_sine = low_ref[:, im]
        high_ref[:, re] = cosine * keep + minus_sine * swap
        high_ref[:, im] = minus_sine * keep - cosine * swap
        spec_ref[:, both] = forward(filt, low_ref, high_ref, both, half)


def filter_spectrum_dense(filt):
    channels, length = filt.shape
    low = half_matrix(length)
    high, spec = call(
        filter_kernel,
        None,
        [
            jax.ShapeDtypeStruct((length // 2, 2 * length), bf16),
            jax.ShapeDtypeStruct((channels, 2 * length), f32),
        ],
        [],
        4 * channels * length * length,
        4 * channels * length * 3 + 4 * length * length,
        VMEM_MIB,
        (filt, low),
    )
    return (low, high), spec


def forward(rows, low_ref, high_ref, cols, half):
    low = jnp.dot(rows[:, :half], low_ref[:, cols], preferred_element_type=f32)
    return low + jnp.dot(rows[:, half:], high_ref[:, cols], preferred_element_type=f32)


def inverse(prod_ref, low_ref, high_ref, start, size):
    half = low_ref.shape[0]
    ref, start = (low_ref, start) if start < half else (high_ref, start - half)
    return lax.dot_general(
        prod_ref[...],
        ref[start : start + size, :],
        (((1,), (1,)), ((), ())),
        preferred_element_type=f32,
    ).astype(bf16)


def multiply_spectra(a_re, a_im, b_re, b_im, first_tile, length):
    rr = a_re * b_re
    ii = a_im * b_im
    cross = a_im * b_re - a_re * b_im
    if not first_tile:
        return (rr + ii) * (1.0 / length), cross * (1.0 / length)
    first = lax.broadcasted_iota(jnp.int32, rr.shape, 1) == 0
    scale = jnp.where(first, 0.5 / length, 1.0 / length)
    return jnp.where(first, rr, rr + ii) * scale, jnp.where(first, ii, cross) * scale


def gather_rows(axis, which, got_refs, rows_ref):
    me = lax.axis_index(axis)
    for k, got_ref in enumerate(got_refs):
        rows_ref[me ^ k] = got_ref[...] if len(got_ref.shape) == 2 else got_ref[which]
    return jnp.concatenate([rows_ref[p] for p in range(len(got_refs))], axis=1)


def correlate_kernel(axis, low_ref, high_ref, filt_spec_ref, *refs):
    count = (len(refs) - 3) // 2
    got_refs, out_refs = refs[:count], refs[count : 2 * count]
    spec_ref, rows_ref, prod_ref = refs[2 * count :]
    block = rows_ref.shape[2]
    length = count * block
    rows = gather_rows(axis, 0, got_refs, rows_ref)
    for n in range(length // LANES):
        re = pl.ds(2 * n * LANES, LANES)
        im = pl.ds((2 * n + 1) * LANES, LANES)
        both = pl.ds(2 * n * LANES, 2 * LANES)
        spec = forward(rows, low_ref, high_ref, both, length // 2)
        spec_ref[:, both] = spec
        real, imag = multiply_spectra(
            spec[:, :LANES], spec[:, LANES:], filt_spec_ref[:, re], filt_spec_ref[:, im], n == 0, length
        )
        prod_ref[:, re] = real.astype(bf16)
        prod_ref[:, im] = imag.astype(bf16)
    pair = 2 * LANES // block
    for q in range(count // pair):
        out = inverse(prod_ref, low_ref, high_ref, q * 2 * LANES, 2 * LANES)
        for part in range(pair):
            rows_ref[q * pair + part] = out[:, part * block : (part + 1) * block]
    me = lax.axis_index(axis)
    for k, out_ref in enumerate(out_refs):
        out_ref[...] = rows_ref[me ^ k]


def correlate_dense(got, w, filt_spec, axis):
    count = len(got)
    channels, block = got[-1].shape
    length = count * block
    *corr, spec = call(
        functools.partial(correlate_kernel, axis),
        None,
        [jax.ShapeDtypeStruct((channels, block), bf16)] * count
        + [jax.ShapeDtypeStruct((channels, 2 * length), f32)],
        [pltpu.VMEM((count, channels, block), bf16), pltpu.VMEM((channels, 2 * length), bf16)],
        8 * channels * length * length,
        4 * length * length + 20 * channels * length,
        VMEM_MIB,
        (*w, filt_spec, *got),
    )
    return corr, spec


def gradient_kernel(axis, share_axis, shares, low_ref, high_ref, grad_spec_ref, *refs):
    count = len(refs) - shares - 3
    got_refs, out_refs = refs[:count], refs[count : count + shares]
    rows_ref, prod_ref, taps_ref = refs[count + shares :]
    length = count * rows_ref.shape[2]
    rows = gather_rows(axis, 1, got_refs, rows_ref)
    for n in range(length // LANES):
        re = pl.ds(2 * n * LANES, LANES)
        im = pl.ds((2 * n + 1) * LANES, LANES)
        both = pl.ds(2 * n * LANES, 2 * LANES)
        spec = forward(rows, low_ref, high_ref, both, length // 2)
        real, imag = multiply_spectra(
            grad_spec_ref[:, re], grad_spec_ref[:, im], spec[:, :LANES], spec[:, LANES:], n == 0, length
        )
        prod_ref[:, re] = real.astype(bf16)
        prod_ref[:, im] = imag.astype(bf16)
    taps = length // shares
    for q in range(shares):
        taps_ref[q] = inverse(prod_ref, low_ref, high_ref, q * taps, taps)
    me = lax.axis_index(share_axis)
    for k, out_ref in enumerate(out_refs):
        out_ref[...] = taps_ref[me ^ k]


def gradient_dense(got, w, grad_spec, axis, share_axis):
    count = len(got)
    shares = lax.axis_size(share_axis)
    channels, block = got[-1].shape
    length = count * block
    return call(
        functools.partial(gradient_kernel, axis, share_axis, shares),
        None,
        [jax.ShapeDtypeStruct((channels, length // shares), bf16)] * shares,
        [
            pltpu.VMEM((count, channels, block), bf16),
            pltpu.VMEM((channels, 2 * length), bf16),
            pltpu.VMEM((shares, channels, length // shares), bf16),
        ],
        8 * channels * length * length,
        4 * length * length + 20 * channels * length,
        VMEM_MIB,
        (*w, grad_spec, *got),
    )


def finish_kernel(axis, shares, scale, base_ref, pr_ref, vb_ref, *refs):
    count = len(refs) - shares - 7
    back_refs, term_refs = refs[:count], refs[count : count + shares]
    pre_out, value_out, grad_out, pre_buf, value_buf, grad_buf, sems = refs[count + shares :]
    rows = back_refs[0].shape[0]
    copies = []

    def send(source, target, sem):
        copy = pltpu.make_async_copy(source, target, sem)
        copy.start()
        copies.append(copy)

    for k, back_ref in enumerate(back_refs):
        block = peer_rows(axis, k, rows)
        summed = back_ref[...].astype(f32) + base_ref[block]
        pre_buf[k] = (summed * vb_ref[block].astype(f32)).astype(bf16)
        value_buf[k] = (summed * pr_ref[block].astype(f32)).astype(bf16)
        send(pre_buf.at[k], pre_out.at[block], sems.at[0, k])
        send(value_buf.at[k], value_out.at[block], sems.at[1, k])
    grad_buf[...] = sum(term_ref[...].astype(f32) for term_ref in term_refs) * scale
    send(grad_buf, grad_out, sems.at[2, 0])
    for copy in copies:
        copy.wait()


def finish(back, base, pre_gate, value_branch, terms, scale, axis):
    count = len(back)
    rows, block = back[0].shape
    channels = count * rows
    return call(
        functools.partial(finish_kernel, axis, len(terms), scale),
        [pl.BlockSpec(memory_space=pltpu.HBM)] * 3,
        [jax.ShapeDtypeStruct((channels, block), bf16)] * 2
        + [jax.ShapeDtypeStruct(terms[0].shape, f32)],
        [
            pltpu.VMEM((count, rows, block), bf16),
            pltpu.VMEM((count, rows, block), bf16),
            pltpu.VMEM(terms[0].shape, f32),
            pltpu.SemaphoreType.DMA((3, count)),
        ],
        3 * channels * block,
        14 * channels * block,
        8,
        (base, pre_gate, value_branch, *back, *terms),
    )


def swap(value, axis, k):
    return lax.ppermute(value, axis, [(j, j ^ k) for j in range(lax.axis_size(axis))])


def peers(count):
    return list(range(count // 2)), list(range(count // 2, count))


def shards_dense(grad_output, post_gate, pre_gate, value_branch, long_filter, skip_weight):
    groups = lax.axis_size("ctx")
    shares = lax.axis_size("dp")
    seqs, channels, block = grad_output.shape
    length = long_filter.shape[1]
    token_count = seqs * shares * length
    near, far = peers(groups)
    rows = [x.reshape(channels, block) for x in (grad_output, post_gate, pre_gate, value_branch)]
    both, gated, saved = product(rows, near, far, "ctx")
    gated = [swap(gated[k], "ctx", k) for k in far]
    both = [both[0]] + [swap(both[k], "ctx", k) for k in near[1:]]
    saved = [swap(saved[k], "ctx", k) for k in far]
    w, filt_spec = filter_spectrum_dense(long_filter)
    own = (rows[0].astype(f32) * rows[1].astype(f32)).astype(bf16)
    base = skip_weight[:, None] * own.astype(f32)
    corr, grad_spec = correlate_dense(both + gated, w, filt_spec, "ctx")
    back = corr[:1] + [swap(corr[k], "ctx", k) for k in range(1, groups)]
    terms = gradient_dense(both + saved, w, grad_spec, "ctx", "dp")
    terms = terms[:1] + [swap(terms[k], "dp", k) for k in range(1, shares)]
    grad_pre_gate, grad_value_branch, grad_long_filter = finish(
        back, base, rows[2], rows[3], terms, 1.0 / math.sqrt(token_count), "ctx"
    )
    shape = grad_output.shape
    return (grad_pre_gate.reshape(shape), grad_value_branch.reshape(shape), grad_long_filter)


def split_factor(length):
    for candidate in range(128, 1, -1):
        if length % candidate == 0:
            return candidate
    return 1


def twiddle(row_count, col_count, modulus, sign_value):
    row_index = lax.broadcasted_iota(jnp.int32, (row_count, col_count), 0)
    col_index = lax.broadcasted_iota(jnp.int32, (row_count, col_count), 1)
    phases = row_index * col_index % modulus
    angles = phases.astype(jnp.float32) * (2.0 * math.pi / modulus)
    return (jnp.cos(angles), sign_value * jnp.sin(angles))


def block_matrix(row_count, col_count, modulus, sign_value, part_count):
    cosine, sine = twiddle(row_count, col_count, modulus, sign_value)
    matrix = jnp.stack([jnp.stack([cosine, sine], 1), jnp.stack([-sine, cosine], 1)], 0)
    return matrix[:part_count]


def transform(parts, sign_value, length):
    part_count = parts.shape[0]
    width = parts.shape[-1]
    leading = split_factor(length)
    if length <= 256 or leading == 1 or leading == length:
        matrix = block_matrix(width, length, length, sign_value, part_count)
        return jnp.einsum("p...j,pjqk->q...k", parts, matrix, precision=highest)
    trailing = length // leading
    live = -(-width // trailing)
    if live * trailing != width:
        extra = [(0, 0)] * (parts.ndim - 1) + [(0, live * trailing - width)]
        parts = jnp.pad(parts, extra)
    batch_dims = parts.shape[1:-1]
    parts = parts.reshape((part_count,) + batch_dims + (live, trailing))
    matrix = block_matrix(live, leading, leading, sign_value, part_count)
    first = jnp.einsum("p...jb,pjqk->q...kb", parts, matrix, precision=highest)
    turn_cos, turn_sin = twiddle(leading, trailing, length, sign_value)
    rotated = jnp.stack(
        [first[0] * turn_cos - first[1] * turn_sin, first[0] * turn_sin + first[1] * turn_cos], 0
    )
    deep = transform(rotated, sign_value, trailing)
    return jnp.swapaxes(deep, -1, -2).reshape((2,) + batch_dims + (length,))


def mirror(values):
    return jnp.roll(jnp.flip(values, -1), 1, -1)


def filter_spectrum(filter_rows):
    length = filter_rows.shape[1]
    spectrum = transform(filter_rows[None], -1.0, 2 * length)
    return (spectrum[0], spectrum[1])


def correlate(grad_rows, saved_rows, filt_real, filt_imag):
    length = grad_rows.shape[2]
    padded = 2 * length
    stacked = jnp.stack([grad_rows.astype(jnp.float32), saved_rows.astype(jnp.float32)], 0)
    spectrum = transform(stacked, -1.0, padded)
    spec_real = spectrum[0]
    spec_imag = spectrum[1]
    flip_real = mirror(spec_real)
    flip_imag = mirror(spec_imag)
    grad_real = 0.5 * (spec_real + flip_real)
    grad_imag = 0.5 * (spec_imag - flip_imag)
    input_real = 0.5 * (spec_imag + flip_imag)
    input_imag = 0.5 * (flip_real - spec_real)
    first_real = filt_real * grad_real + filt_imag * grad_imag
    first_imag = filt_real * grad_imag - filt_imag * grad_real
    second_real = grad_real * input_real + grad_imag * input_imag
    second_imag = grad_imag * input_real - grad_real * input_imag
    combined = jnp.stack([first_real - second_imag, first_imag + second_real], 0)
    result = transform(combined, 1.0, padded)
    factor = 1.0 / padded
    correlated = (result[0, ..., :length] * factor).astype(jnp.bfloat16)
    filter_terms = result[1, ..., :length] * factor
    return (correlated, filter_terms)


def shards_long(grad_output, post_gate, pre_gate, value_branch, long_filter, skip_weight):
    seq_count = grad_output.shape[0]
    length = long_filter.shape[1]
    token_count = seq_count * lax.axis_size("dp") * length
    gated = (grad_output.astype(jnp.float32) * post_gate.astype(jnp.float32)).astype(jnp.bfloat16)
    saved = (pre_gate.astype(jnp.float32) * value_branch.astype(jnp.float32)).astype(jnp.bfloat16)
    filt_real, filt_imag = filter_spectrum(long_filter)
    correlated, filter_terms = correlate(
        lax.all_to_all(gated, "ctx", split_axis=1, concat_axis=2, tiled=True),
        lax.all_to_all(saved, "ctx", split_axis=1, concat_axis=2, tiled=True),
        filt_real,
        filt_imag,
    )
    back = lax.all_to_all(correlated, "ctx", split_axis=2, concat_axis=1, tiled=True)
    returned, filter_terms = (back, filter_terms)
    filter_sum = jnp.sum(filter_terms, axis=0)
    shares = lax.psum_scatter(
        filter_sum.astype(jnp.bfloat16), "dp", scatter_dimension=1, tiled=True
    ).astype(jnp.float32)
    summed = returned.astype(jnp.float32) + skip_weight[None, :, None] * gated.astype(jnp.float32)
    grad_pre_gate = (summed * value_branch.astype(jnp.float32)).astype(jnp.bfloat16)
    grad_value_branch = (summed * pre_gate.astype(jnp.float32)).astype(jnp.bfloat16)
    grad_long_filter = shares * (1.0 / math.sqrt(token_count))
    return (grad_pre_gate, grad_value_branch, grad_long_filter)


def shards(grad_output, post_gate, pre_gate, value_branch, long_filter, skip_weight):
    seqs, _, block = grad_output.shape
    rows, length = long_filter.shape
    groups = lax.axis_size("ctx")
    shares = lax.axis_size("dp")
    dense = (
        seqs == 1
        and length <= 1024
        and block == LANES
        and rows % 16 == 0
        and length % (2 * LANES * shares) == 0
        and length % (4 * LANES) == 0
        and groups & (groups - 1) == 0
        and shares & (shares - 1) == 0
        and groups > 2
    )
    body = shards_dense if dense else shards_long
    return body(grad_output, post_gate, pre_gate, value_branch, long_filter, skip_weight)


def solution(mesh):
    return jax.shard_map(
        shards,
        mesh=mesh,
        in_specs=(
            P("dp", None, "ctx"),
            P("dp", None, "ctx"),
            P("dp", None, "ctx"),
            P("dp", None, "ctx"),
            P("ctx", None),
            P(),
        ),
        out_specs=(P("dp", None, "ctx"), P("dp", None, "ctx"), P("ctx", "dp")),
        check_vma=False,
    )
```

profile of v0, /device:TPU:0, one launch (start us, length us, event | category | flops | bytes accessed | tf_op | source)
XLA Modules:
  0.0 53.7 jit_solution(9286296594792610826)
XLA Ops:
  0.6 2.0 %shard_map.95 = (bf16[2,256,128]{2,1,0:T(8,128)(2,1)S(1)}, bf16[2,256,128]{2,1,0:T(8,128)(2,1)S(1)}, bf16[2,256,128]{2,1,0:T(8,128)(2,1)S(1)}, bf16[2,256,128]{2...) custom-call(bf16[2048,128]{1,0:T(8,128)(2,1)} %bitcast.13, ...), custom_call_target="tpu_custom_call" | custom-call | flops 524288 | bytes 3145728 | tf_op jit(solution)/shard_map/pallas_call | solution.py:39
  2.6 4.1 %collective-permute-start.3 = (bf16[256,128]{1,0:T(8,128)(2,1)S(1)}, bf16[256,128]{1,0:T(8,128)(2,1)S(1)}, u32[]{:S(2)}, u32[]{:S(2)}) collective-permute-start(bf16[256,128]{1,0:T(8,128)(2,1)S(1)} %get-tuple-element.39), channel_id=1, source_target_pairs={{0,4},{1,5},{2,6},{3,7},{4,0},{5,1},{6,2},{7,3},{8,12},{9,13},{10,... | collective-permute-start | bytes 196616 | tf_op jit(solution)/shard_map/ppermute | solution.py:310
  6.7 1.3 %collective-permute-start.4 = (bf16[256,128]{1,0:T(8,128)(2,1)S(1)}, bf16[256,128]{1,0:T(8,128)(2,1)S(1)}, u32[]{:S(2)}, u32[]{:S(2)}) collective-permute-start(bf16[256,128]{1,0:T(8,128)(2,1)S(1)} %get-tuple-element.40), channel_id=1, source_target_pairs={{0,5},{1,4},{2,7},{3,6},{4,1},{5,0},{6,3},{7,2},{8,13},{9,12},{10,... | collective-permute-start | bytes 196616 | tf_op jit(solution)/shard_map/ppermute | solution.py:310
  8.0 0.2 collective-permute-start
  8.3 1.8 %collective-permute-start.1 = (bf16[2,256,128]{2,1,0:T(8,128)(2,1)S(1)}, bf16[2,256,128]{2,1,0:T(8,128)(2,1)S(1)}, u32[]{:S(2)}, u32[]{:S(2)}) collective-permute-start(bf16[2,256,128]{2,1,0:T(8,128)(2,1)S(1)} %get-tuple-element.37), channel_id=1, source_target_pairs={{0,2},{1,3},{2,0},{3,1},{4,6},{5,7},{6,4},{7,5},{8,10},{9,11},{10,... | collective-permute-start | bytes 393224 | tf_op jit(solution)/shard_map/ppermute | solution.py:310
  10.1 1.4 %collective-permute-start.2 = (bf16[2,256,128]{2,1,0:T(8,128)(2,1)S(1)}, bf16[2,256,128]{2,1,0:T(8,128)(2,1)S(1)}, u32[]{:S(2)}, u32[]{:S(2)}) collective-permute-start(bf16[2,256,128]{2,1,0:T(8,128)(2,1)S(1)} %get-tuple-element.38), channel_id=1, source_target_pairs={{0,3},{1,2},{2,1},{3,0},{4,7},{5,6},{6,5},{7,4},{8,11},{9,10},{10,... | collective-permute-start | bytes 393224 | tf_op jit(solution)/shard_map/ppermute | solution.py:310
  11.5 0.0 collective-permute-done.3.refs_4_
  11.5 4.1 %collective-permute-start.5 = (bf16[256,128]{1,0:T(8,128)(2,1)S(1)}, bf16[256,128]{1,0:T(8,128)(2,1)S(1)}, u32[]{:S(2)}, u32[]{:S(2)}) collective-permute-start(bf16[256,128]{1,0:T(8,128)(2,1)S(1)} %get-tuple-element.41), channel_id=1, source_target_pairs={{0,6},{1,7},{2,4},{3,5},{4,2},{5,3},{6,0},{7,1},{8,14},{9,15},{10,... | collective-permute-start | bytes 196616 | tf_op jit(solution)/shard_map/ppermute | solution.py:310
  15.6 0.0 collective-permute-done.4.refs_5_
  15.6 2.2 %collective-permute-start.6 = (bf16[256,128]{1,0:T(8,128)(2,1)S(1)}, bf16[256,128]{1,0:T(8,128)(2,1)S(1)}, u32[]{:S(2)}, u32[]{:S(2)}) collective-permute-start(bf16[256,128]{1,0:T(8,128)(2,1)S(1)} %get-tuple-element.42), channel_id=1, source_target_pairs={{0,7},{1,6},{2,5},{3,4},{4,3},{5,2},{6,1},{7,0},{8,15},{9,14},{10,... | collective-permute-start | bytes 196616 | tf_op jit(solution)/shard_map/ppermute | solution.py:310
  17.9 1.6 %copy-done.3 = bf16[512,2048]{1,0:T(8,128)(2,1)S(1)} copy-done((bf16[512,2048]{1,0:T(8,128)(2,1)S(1)}, bf16[512,2048]{1,0:T(8,128)(2,1)}, u32[]{:S(2)}) %copy-start.3) | copy-done | bytes 2097176
  19.4 1.4 %shard_map.94 = (bf16[512,2048]{1,0:T(8,128)(2,1)S(1)}, f32[256,2048]{1,0:T(8,128)S(1)}) custom-call(f32[256,1024]{1,0:T(8,128)S(1)} %copy-done.2, bf16[512,2048]{1,0:T(8,128)(2,1)S(1)} %copy-done.3), custom_call_target="tpu_custom_call" | custom-call | flops 1073741824 | bytes 7340032 | tf_op jit(solution)/shard_map/pallas_call | solution.py:39
  20.9 0.0 collective-permute-done.5.refs_6_
  20.9 0.1 collective-permute-start.14
  20.9 1.6 %collective-permute-done.6.refs_7_ = bf16[256,128]{1,0:T(8,128)(2,1)S(1)} collective-permute-done((bf16[256,128]{1,0:T(8,128)(2,1)S(1)}, bf16[256,128]{1,0:T(8,128)(2,1)S(1)}, u32[]{:S(2)}, u32[]{:S(2)}) %collective-permute-start.6) | collective-permute-done | bytes 65568 | tf_op jit(solution)/shard_map/ppermute | solution.py:310
  22.6 2.1 %collective-permute-start.15 = (bf16[256,128]{1,0:T(8,128)(2,1)S(1)}, bf16[256,128]{1,0:T(8,128)(2,1)S(1)}, u32[]{:S(2)}, u32[]{:S(2)}) collective-permute-start(bf16[256,128]{1,0:T(8,128)(2,1)S(1)} %get-tuple-element.53), channel_id=1, source_target_pairs={{0,5},{1,4},{2,7},{3,6},{4,1},{5,0},{6,3},{7,2},{8,13},{9,12},{10,... | collective-permute-start | bytes 196616 | tf_op jit(solution)/shard_map/ppermute | solution.py:310
  24.6 0.0 collective-permute-done.refs_1_
  24.6 1.7 %collective-permute-start.16 = (bf16[256,128]{1,0:T(8,128)(2,1)S(1)}, bf16[256,128]{1,0:T(8,128)(2,1)S(1)}, u32[]{:S(2)}, u32[]{:S(2)}) collective-permute-start(bf16[256,128]{1,0:T(8,128)(2,1)S(1)} %get-tuple-element.54), channel_id=1, source_target_pairs={{0,6},{1,7},{2,4},{3,5},{4,2},{5,3},{6,0},{7,1},{8,14},{9,15},{10,... | collective-permute-start | bytes 196616 | tf_op jit(solution)/shard_map/ppermute | solution.py:310
  26.3 0.0 collective-permute-done.1.refs_2_
  26.3 2.2 %collective-permute-start.17 = (bf16[256,128]{1,0:T(8,128)(2,1)S(1)}, bf16[256,128]{1,0:T(8,128)(2,1)S(1)}, u32[]{:S(2)}, u32[]{:S(2)}) collective-permute-start(bf16[256,128]{1,0:T(8,128)(2,1)S(1)} %get-tuple-element.55), channel_id=1, source_target_pairs={{0,7},{1,6},{2,5},{3,4},{4,3},{5,2},{6,1},{7,0},{8,15},{9,14},{10,... | collective-permute-start | bytes 196616 | tf_op jit(solution)/shard_map/ppermute | solution.py:310
  28.6 0.0 collective-permute-done.2.refs_3_
  28.6 2.5 %shard_map.96 = (bf16[256,128]{1,0:T(8,128)(2,1)S(1)}, bf16[256,128]{1,0:T(8,128)(2,1)S(1)}, bf16[256,128]{1,0:T(8,128)(2,1)S(1)}, bf16[256,128]{1,0:T(8,128)(2,...) custom-call(bf16[512,2048]{1,0:T(8,128)(2,1)S(1)} %copy-done.4, ...), custom_call_target="tpu_custom_call" | custom-call | flops 2147483648 | bytes 9437184 | tf_op jit(solution)/shard_map/pallas_call | solution.py:39
  31.1 0.1 collective-permute-start.10
  31.2 0.0 collective-permute-done.14.refs_4_
  31.2 3.7 %collective-permute-start.11 = (bf16[256,128]{1,0:T(8,128)(2,1)S(1)}, bf16[256,128]{1,0:T(8,128)(2,1)S(1)}, u32[]{:S(2)}, u32[]{:S(2)}) collective-permute-start(bf16[256,128]{1,0:T(8,128)(2,1)S(1)} %get-tuple-element.48), channel_id=1, source_target_pairs={{0,5},{1,4},{2,7},{3,6},{4,1},{5,0},{6,3},{7,2},{8,13},{9,12},{10,... | collective-permute-start | bytes 196616 | tf_op jit(solution)/shard_map/ppermute | solution.py:310
  34.9 0.0 collective-permute-done.15.refs_5_
  34.9 1.7 %collective-permute-start.12 = (bf16[256,128]{1,0:T(8,128)(2,1)S(1)}, bf16[256,128]{1,0:T(8,128)(2,1)S(1)}, u32[]{:S(2)}, u32[]{:S(2)}) collective-permute-start(bf16[256,128]{1,0:T(8,128)(2,1)S(1)} %get-tuple-element.49), channel_id=1, source_target_pairs={{0,6},{1,7},{2,4},{3,5},{4,2},{5,3},{6,0},{7,1},{8,14},{9,15},{10,... | collective-permute-start | bytes 196616 | tf_op jit(solution)/shard_map/ppermute | solution.py:310
  36.6 0.0 collective-permute-done.16.refs_6_
  36.6 2.2 %collective-permute-start.13 = (bf16[256,128]{1,0:T(8,128)(2,1)S(1)}, bf16[256,128]{1,0:T(8,128)(2,1)S(1)}, u32[]{:S(2)}, u32[]{:S(2)}) collective-permute-start(bf16[256,128]{1,0:T(8,128)(2,1)S(1)} %get-tuple-element.50), channel_id=1, source_target_pairs={{0,7},{1,6},{2,5},{3,4},{4,3},{5,2},{6,1},{7,0},{8,15},{9,14},{10,... | collective-permute-start | bytes 196616 | tf_op jit(solution)/shard_map/ppermute | solution.py:310
  38.8 0.0 collective-permute-done.17.refs_7_
  38.8 1.3 %collective-permute-start.7 = (bf16[256,128]{1,0:T(8,128)(2,1)S(1)}, bf16[256,128]{1,0:T(8,128)(2,1)S(1)}, u32[]{:S(2)}, u32[]{:S(2)}) collective-permute-start(bf16[256,128]{1,0:T(8,128)(2,1)S(1)} %get-tuple-element.44), channel_id=1, source_target_pairs={{0,1},{1,0},{2,3},{3,2},{4,5},{5,4},{6,7},{7,6},{8,9},{9,8},{10,11... | collective-permute-start | bytes 196616 | tf_op jit(solution)/shard_map/ppermute | solution.py:310
  40.2 2.5 %shard_map.97 = (bf16[256,256]{1,0:T(8,128)(2,1)S(1)}, bf16[256,256]{1,0:T(8,128)(2,1)S(1)}, bf16[256,256]{1,0:T(8,128)(2,1)S(1)}, bf16[256,256]{1,0:T(8,128)(2,1)S(1)}) custom-call(bf16[512,2048]{1,0:T(8,128)(2,1)S(1)} %copy-done.4, bf16[512,2048]{1,0:T(8,128)(2,1)S(1)} %get-tuple-element.33.high_ref, f32[256,2048]{1,0:T(8,128)S(1)} %get-tuple-element.51.grad_spec_ref, ...), custom_call_target="tpu_custom_call" | custom-call | flops 2147483648 | bytes 9437184 | tf_op jit(solution)/shard_map/pallas_call | solution.py:39
  42.7 0.0 copy-start
  42.7 0.0 copy-start.1
  42.7 0.0 collective-permute-done.10.refs_4_
  42.7 0.1 collective-permute-start.18
  42.8 1.6 %collective-permute-done.11.refs_5_ = bf16[256,128]{1,0:T(8,128)(2,1)S(1)} collective-permute-done((bf16[256,128]{1,0:T(8,128)(2,1)S(1)}, bf16[256,128]{1,0:T(8,128)(2,1)S(1)}, u32[]{:S(2)}, u32[]{:S(2)}) %collective-permute-start.11) | collective-permute-done | bytes 65568 | tf_op jit(solution)/shard_map/ppermute | solution.py:310
  44.4 1.5 %collective-permute-start.19 = (bf16[256,256]{1,0:T(8,128)(2,1)S(1)}, bf16[256,256]{1,0:T(8,128)(2,1)S(1)}, u32[]{:S(2)}, u32[]{:S(2)}) collective-permute-start(bf16[256,256]{1,0:T(8,128)(2,1)S(1)} %get-tuple-element.58), channel_id=1, source_target_pairs={{0,16},{8,24},{16,0},{24,8},{1,17},{9,25},{17,1},{25,9},{2,18},{10... | collective-permute-start | bytes 393224 | tf_op jit(solution)/shard_map/ppermute | solution.py:310
  45.9 0.0 collective-permute-done.12.refs_6_
  45.9 0.0 collective-permute-start.20
  45.9 1.2 %collective-permute-start.8 = (bf16[256,128]{1,0:T(8,128)(2,1)S(1)}, bf16[256,128]{1,0:T(8,128)(2,1)S(1)}, u32[]{:S(2)}, u32[]{:S(2)}) collective-permute-start(bf16[256,128]{1,0:T(8,128)(2,1)S(1)} %get-tuple-element.45), channel_id=1, source_target_pairs={{0,2},{1,3},{2,0},{3,1},{4,6},{5,7},{6,4},{7,5},{8,10},{9,11},{10,... | collective-permute-start | bytes 196616 | tf_op jit(solution)/shard_map/ppermute | solution.py:310
  47.1 1.3 %collective-permute-start.9 = (bf16[256,128]{1,0:T(8,128)(2,1)S(1)}, bf16[256,128]{1,0:T(8,128)(2,1)S(1)}, u32[]{:S(2)}, u32[]{:S(2)}) collective-permute-start(bf16[256,128]{1,0:T(8,128)(2,1)S(1)} %get-tuple-element.46), channel_id=1, source_target_pairs={{0,3},{1,2},{2,1},{3,0},{4,7},{5,6},{6,5},{7,4},{8,11},{9,10},{10,... | collective-permute-start | bytes 196616 | tf_op jit(solution)/shard_map/ppermute | solution.py:310
  48.4 0.3 convert_multiply_fusion.base_ref
  48.8 2.1 %collective-permute-done.8.refs_2_ = bf16[256,128]{1,0:T(8,128)(2,1)S(1)} collective-permute-done((bf16[256,128]{1,0:T(8,128)(2,1)S(1)}, bf16[256,128]{1,0:T(8,128)(2,1)S(1)}, u32[]{:S(2)}, u32[]{:S(2)}) %collective-permute-start.8) | collective-permute-done | bytes 65568 | tf_op jit(solution)/shard_map/ppermute | solution.py:310
  50.8 1.5 %collective-permute-done.9.refs_3_ = bf16[256,128]{1,0:T(8,128)(2,1)S(1)} collective-permute-done((bf16[256,128]{1,0:T(8,128)(2,1)S(1)}, bf16[256,128]{1,0:T(8,128)(2,1)S(1)}, u32[]{:S(2)}, u32[]{:S(2)}) %collective-permute-start.9) | collective-permute-done | bytes 65568 | tf_op jit(solution)/shard_map/ppermute | solution.py:310
  52.4 0.0 collective-permute-done.18.refs_9_
  52.4 0.0 collective-permute-done.19.refs_10_
  52.4 1.3 %shard_map.98 = (bf16[2048,128]{1,0:T(8,128)(2,1)}, bf16[2048,128]{1,0:T(8,128)(2,1)}, f32[256,256]{1,0:T(8,128)}) custom-call(f32[2048,128]{1,0:T(8,128)S(1)} %convert_multiply_fusion.base_ref, bf16[2048,128]{1,0:T(8,128)(2,1)S(1)} %bitcast.9, bf16[2048,128]{1,0:T(8,128)(2,1)S(1)} %bitcast.11, bf16[256,128]{1,0:T(8,128)(2,1)S(1)} %get-tuple-element.43.refs_0_, ...), custom_call_target="tpu_custom_call" | custom-call | flops 786432 | bytes 3670016 | tf_op jit(solution)/shard_map/pallas_call | solution.py:39
  (16 shorter events, 0.0 us)
Async XLA Ops:
  0.6 17.2 %copy-start.2 = (f32[256,1024]{1,0:T(8,128)S(1)}, f32[256,1024]{1,0:T(8,128)}, u32[]{:S(2)}) copy-start(f32[256,1024]{1,0:T(8,128)} %filt_ref.1) | copy-start | bytes 3145732
  2.6 8.9 %collective-permute-start.3 = (bf16[256,128]{1,0:T(8,128)(2,1)S(1)}, bf16[256,128]{1,0:T(8,128)(2,1)S(1)}, u32[]{:S(2)}, u32[]{:S(2)}) collective-permute-start(bf16[256,128]{1,0:T(8,128)(2,1)S(1)} %get-tuple-element.39), channel_id=1, source_target_pairs={{0,4},{1,5},{2,6},{3,7},{4,0},{5,1},{6,2},{7,3},{8,12},{9,13},{10,... | collective-permute-start | bytes 196616 | tf_op jit(solution)/shard_map/ppermute | solution.py:310
  6.7 8.9 %collective-permute-start.4 = (bf16[256,128]{1,0:T(8,128)(2,1)S(1)}, bf16[256,128]{1,0:T(8,128)(2,1)S(1)}, u32[]{:S(2)}, u32[]{:S(2)}) collective-permute-start(bf16[256,128]{1,0:T(8,128)(2,1)S(1)} %get-tuple-element.40), channel_id=1, source_target_pairs={{0,5},{1,4},{2,7},{3,6},{4,1},{5,0},{6,3},{7,2},{8,13},{9,12},{10,... | collective-permute-start | bytes 196616 | tf_op jit(solution)/shard_map/ppermute | solution.py:310
  8.0 16.6 %collective-permute-start = (bf16[2,256,128]{2,1,0:T(8,128)(2,1)S(1)}, bf16[2,256,128]{2,1,0:T(8,128)(2,1)S(1)}, u32[]{:S(2)}, u32[]{:S(2)}) collective-permute-start(bf16[2,256,128]{2,1,0:T(8,128)(2,1)S(1)} %get-tuple-element.36), channel_id=1, source_target_pairs={{0,1},{1,0},{2,3},{3,2},{4,5},{5,4},{6,7},{7,6},{8,9},{9,8},{10,11... | collective-permute-start | bytes 393224 | tf_op jit(solution)/shard_map/ppermute | solution.py:310
  8.3 18.1 %collective-permute-start.1 = (bf16[2,256,128]{2,1,0:T(8,128)(2,1)S(1)}, bf16[2,256,128]{2,1,0:T(8,128)(2,1)S(1)}, u32[]{:S(2)}, u32[]{:S(2)}) collective-permute-start(bf16[2,256,128]{2,1,0:T(8,128)(2,1)S(1)} %get-tuple-element.37), channel_id=1, source_target_pairs={{0,2},{1,3},{2,0},{3,1},{4,6},{5,7},{6,4},{7,5},{8,10},{9,11},{10,... | collective-permute-start | bytes 393224 | tf_op jit(solution)/shard_map/ppermute | solution.py:310
  10.1 18.5 %collective-permute-start.2 = (bf16[2,256,128]{2,1,0:T(8,128)(2,1)S(1)}, bf16[2,256,128]{2,1,0:T(8,128)(2,1)S(1)}, u32[]{:S(2)}, u32[]{:S(2)}) collective-permute-start(bf16[2,256,128]{2,1,0:T(8,128)(2,1)S(1)} %get-tuple-element.38), channel_id=1, source_target_pairs={{0,3},{1,2},{2,1},{3,0},{4,7},{5,6},{6,5},{7,4},{8,11},{9,10},{10,... | collective-permute-start | bytes 393224 | tf_op jit(solution)/shard_map/ppermute | solution.py:310
  11.5 9.3 %collective-permute-start.5 = (bf16[256,128]{1,0:T(8,128)(2,1)S(1)}, bf16[256,128]{1,0:T(8,128)(2,1)S(1)}, u32[]{:S(2)}, u32[]{:S(2)}) collective-permute-start(bf16[256,128]{1,0:T(8,128)(2,1)S(1)} %get-tuple-element.41), channel_id=1, source_target_pairs={{0,6},{1,7},{2,4},{3,5},{4,2},{5,3},{6,0},{7,1},{8,14},{9,15},{10,... | collective-permute-start | bytes 196616 | tf_op jit(solution)/shard_map/ppermute | solution.py:310
  15.6 7.0 %collective-permute-start.6 = (bf16[256,128]{1,0:T(8,128)(2,1)S(1)}, bf16[256,128]{1,0:T(8,128)(2,1)S(1)}, u32[]{:S(2)}, u32[]{:S(2)}) collective-permute-start(bf16[256,128]{1,0:T(8,128)(2,1)S(1)} %get-tuple-element.42), channel_id=1, source_target_pairs={{0,7},{1,6},{2,5},{3,4},{4,3},{5,2},{6,1},{7,0},{8,15},{9,14},{10,... | collective-permute-start | bytes 196616 | tf_op jit(solution)/shard_map/ppermute | solution.py:310
  17.9 1.6 %copy-start.3 = (bf16[512,2048]{1,0:T(8,128)(2,1)S(1)}, bf16[512,2048]{1,0:T(8,128)(2,1)}, u32[]{:S(2)}) copy-start(bf16[512,2048]{1,0:T(8,128)(2,1)} %constant.2.clone.low_ref) | copy-start | bytes 6291460
  19.4 9.2 %copy-start.4 = (bf16[512,2048]{1,0:T(8,128)(2,1)S(1)}, bf16[512,2048]{1,0:T(8,128)(2,1)}, u32[]{:S(2)}) copy-start(bf16[512,2048]{1,0:T(8,128)(2,1)} %constant.2.clone.low_ref) | copy-start | bytes 6291460
  20.9 10.3 %collective-permute-start.14 = (bf16[256,128]{1,0:T(8,128)(2,1)S(1)}, bf16[256,128]{1,0:T(8,128)(2,1)S(1)}, u32[]{:S(2)}, u32[]{:S(2)}) collective-permute-start(bf16[256,128]{1,0:T(8,128)(2,1)S(1)} %get-tuple-element.52), channel_id=1, source_target_pairs={{0,4},{1,5},{2,6},{3,7},{4,0},{5,1},{6,2},{7,3},{8,12},{9,13},{10,... | collective-permute-start | bytes 196616 | tf_op jit(solution)/shard_map/ppermute | solution.py:310
  22.6 12.3 %collective-permute-start.15 = (bf16[256,128]{1,0:T(8,128)(2,1)S(1)}, bf16[256,128]{1,0:T(8,128)(2,1)S(1)}, u32[]{:S(2)}, u32[]{:S(2)}) collective-permute-start(bf16[256,128]{1,0:T(8,128)(2,1)S(1)} %get-tuple-element.53), channel_id=1, source_target_pairs={{0,5},{1,4},{2,7},{3,6},{4,1},{5,0},{6,3},{7,2},{8,13},{9,12},{10,... | collective-permute-start | bytes 196616 | tf_op jit(solution)/shard_map/ppermute | solution.py:310
  24.6 11.9 %collective-permute-start.16 = (bf16[256,128]{1,0:T(8,128)(2,1)S(1)}, bf16[256,128]{1,0:T(8,128)(2,1)S(1)}, u32[]{:S(2)}, u32[]{:S(2)}) collective-permute-start(bf16[256,128]{1,0:T(8,128)(2,1)S(1)} %get-tuple-element.54), channel_id=1, source_target_pairs={{0,6},{1,7},{2,4},{3,5},{4,2},{5,3},{6,0},{7,1},{8,14},{9,15},{10,... | collective-permute-start | bytes 196616 | tf_op jit(solution)/shard_map/ppermute | solution.py:310
  26.3 12.5 %collective-permute-start.17 = (bf16[256,128]{1,0:T(8,128)(2,1)S(1)}, bf16[256,128]{1,0:T(8,128)(2,1)S(1)}, u32[]{:S(2)}, u32[]{:S(2)}) collective-permute-start(bf16[256,128]{1,0:T(8,128)(2,1)S(1)} %get-tuple-element.55), channel_id=1, source_target_pairs={{0,7},{1,6},{2,5},{3,4},{4,3},{5,2},{6,1},{7,0},{8,15},{9,14},{10,... | collective-permute-start | bytes 196616 | tf_op jit(solution)/shard_map/ppermute | solution.py:310
  31.1 11.6 %collective-permute-start.10 = (bf16[256,128]{1,0:T(8,128)(2,1)S(1)}, bf16[256,128]{1,0:T(8,128)(2,1)S(1)}, u32[]{:S(2)}, u32[]{:S(2)}) collective-permute-start(bf16[256,128]{1,0:T(8,128)(2,1)S(1)} %get-tuple-element.47), channel_id=1, source_target_pairs={{0,4},{1,5},{2,6},{3,7},{4,0},{5,1},{6,2},{7,3},{8,12},{9,13},{10,... | collective-permute-start | bytes 196616 | tf_op jit(solution)/shard_map/ppermute | solution.py:310
  31.2 13.2 %collective-permute-start.11 = (bf16[256,128]{1,0:T(8,128)(2,1)S(1)}, bf16[256,128]{1,0:T(8,128)(2,1)S(1)}, u32[]{:S(2)}, u32[]{:S(2)}) collective-permute-start(bf16[256,128]{1,0:T(8,128)(2,1)S(1)} %get-tuple-element.48), channel_id=1, source_target_pairs={{0,5},{1,4},{2,7},{3,6},{4,1},{5,0},{6,3},{7,2},{8,13},{9,12},{10,... | collective-permute-start | bytes 196616 | tf_op jit(solution)/shard_map/ppermute | solution.py:310
  34.9 11.1 %collective-permute-start.12 = (bf16[256,128]{1,0:T(8,128)(2,1)S(1)}, bf16[256,128]{1,0:T(8,128)(2,1)S(1)}, u32[]{:S(2)}, u32[]{:S(2)}) collective-permute-start(bf16[256,128]{1,0:T(8,128)(2,1)S(1)} %get-tuple-element.49), channel_id=1, source_target_pairs={{0,6},{1,7},{2,4},{3,5},{4,2},{5,3},{6,0},{7,1},{8,14},{9,15},{10,... | collective-permute-start | bytes 196616 | tf_op jit(solution)/shard_map/ppermute | solution.py:310
  36.6 9.4 %collective-permute-start.13 = (bf16[256,128]{1,0:T(8,128)(2,1)S(1)}, bf16[256,128]{1,0:T(8,128)(2,1)S(1)}, u32[]{:S(2)}, u32[]{:S(2)}) collective-permute-start(bf16[256,128]{1,0:T(8,128)(2,1)S(1)} %get-tuple-element.50), channel_id=1, source_target_pairs={{0,7},{1,6},{2,5},{3,4},{4,3},{5,2},{6,1},{7,0},{8,15},{9,14},{10,... | collective-permute-start | bytes 196616 | tf_op jit(solution)/shard_map/ppermute | solution.py:310
  38.8 8.3 %collective-permute-start.7 = (bf16[256,128]{1,0:T(8,128)(2,1)S(1)}, bf16[256,128]{1,0:T(8,128)(2,1)S(1)}, u32[]{:S(2)}, u32[]{:S(2)}) collective-permute-start(bf16[256,128]{1,0:T(8,128)(2,1)S(1)} %get-tuple-element.44), channel_id=1, source_target_pairs={{0,1},{1,0},{2,3},{3,2},{4,5},{5,4},{6,7},{7,6},{8,9},{9,8},{10,11... | collective-permute-start | bytes 196616 | tf_op jit(solution)/shard_map/ppermute | solution.py:310
  40.2 8.2 %copy-start.5 = (bf16[1,2048,128]{2,1,0:T(8,128)(2,1)S(1)}, bf16[1,2048,128]{2,1,0:T(8,128)(2,1)}, u32[]{:S(2)}) copy-start(bf16[1,2048,128]{2,1,0:T(8,128)(2,1)} %param.8) | copy-start | bytes 1572868
  40.2 8.2 %copy-start.6 = (bf16[1,2048,128]{2,1,0:T(8,128)(2,1)S(1)}, bf16[1,2048,128]{2,1,0:T(8,128)(2,1)}, u32[]{:S(2)}) copy-start(bf16[1,2048,128]{2,1,0:T(8,128)(2,1)} %param.7) | copy-start | bytes 1572868
  40.2 8.2 %copy-start.7 = (f32[2048]{0:T(1024)S(1)}, f32[2048]{0:T(1024)}, u32[]{:S(2)}) copy-start(f32[2048]{0:T(1024)} %param.12) | copy-start | bytes 24580
  42.7 9.7 %copy-start = (bf16[1,2048,128]{2,1,0:T(8,128)(2,1)S(1)}, bf16[1,2048,128]{2,1,0:T(8,128)(2,1)}, u32[]{:S(2)}) copy-start(bf16[1,2048,128]{2,1,0:T(8,128)(2,1)} %param.9) | copy-start | bytes 1572868
  42.7 9.7 %copy-start.1 = (bf16[1,2048,128]{2,1,0:T(8,128)(2,1)S(1)}, bf16[1,2048,128]{2,1,0:T(8,128)(2,1)}, u32[]{:S(2)}) copy-start(bf16[1,2048,128]{2,1,0:T(8,128)(2,1)} %param.10) | copy-start | bytes 1572868
  42.7 9.6 %collective-permute-start.18 = (bf16[256,256]{1,0:T(8,128)(2,1)S(1)}, bf16[256,256]{1,0:T(8,128)(2,1)S(1)}, u32[]{:S(2)}, u32[]{:S(2)}) collective-permute-start(bf16[256,256]{1,0:T(8,128)(2,1)S(1)} %get-tuple-element.57), channel_id=1, source_target_pairs={{0,8},{8,0},{16,24},{24,16},{1,9},{9,1},{17,25},{25,17},{2,10},{10... | collective-permute-start | bytes 393224 | tf_op jit(solution)/shard_map/ppermute | solution.py:310
  44.4 7.9 %collective-permute-start.19 = (bf16[256,256]{1,0:T(8,128)(2,1)S(1)}, bf16[256,256]{1,0:T(8,128)(2,1)S(1)}, u32[]{:S(2)}, u32[]{:S(2)}) collective-permute-start(bf16[256,256]{1,0:T(8,128)(2,1)S(1)} %get-tuple-element.58), channel_id=1, source_target_pairs={{0,16},{8,24},{16,0},{24,8},{1,17},{9,25},{17,1},{25,9},{2,18},{10... | collective-permute-start | bytes 393224 | tf_op jit(solution)/shard_map/ppermute | solution.py:310
  45.9 6.4 %collective-permute-start.20 = (bf16[256,256]{1,0:T(8,128)(2,1)S(1)}, bf16[256,256]{1,0:T(8,128)(2,1)S(1)}, u32[]{:S(2)}, u32[]{:S(2)}) collective-permute-start(bf16[256,256]{1,0:T(8,128)(2,1)S(1)} %get-tuple-element.59), channel_id=1, source_target_pairs={{0,24},{8,16},{16,8},{24,0},{1,25},{9,17},{17,9},{25,1},{2,26},{10... | collective-permute-start | bytes 393224 | tf_op jit(solution)/shard_map/ppermute | solution.py:310
  45.9 4.9 %collective-permute-start.8 = (bf16[256,128]{1,0:T(8,128)(2,1)S(1)}, bf16[256,128]{1,0:T(8,128)(2,1)S(1)}, u32[]{:S(2)}, u32[]{:S(2)}) collective-permute-start(bf16[256,128]{1,0:T(8,128)(2,1)S(1)} %get-tuple-element.45), channel_id=1, source_target_pairs={{0,2},{1,3},{2,0},{3,1},{4,6},{5,7},{6,4},{7,5},{8,10},{9,11},{10,... | collective-permute-start | bytes 196616 | tf_op jit(solution)/shard_map/ppermute | solution.py:310
  47.1 5.2 %collective-permute-start.9 = (bf16[256,128]{1,0:T(8,128)(2,1)S(1)}, bf16[256,128]{1,0:T(8,128)(2,1)S(1)}, u32[]{:S(2)}, u32[]{:S(2)}) collective-permute-start(bf16[256,128]{1,0:T(8,128)(2,1)S(1)} %get-tuple-element.46), channel_id=1, source_target_pairs={{0,3},{1,2},{2,1},{3,0},{4,7},{5,6},{6,5},{7,4},{8,11},{9,10},{10,... | collective-permute-start | bytes 196616 | tf_op jit(solution)/shard_map/ppermute | solution.py:310
where the time goes:
time: 53.8 us; the launch traced here: 53.7 us
  starting transfers between devices  34.4 us (64%)
  Pallas kernels  9.66 us (18%)
  waiting for transfers between devices  6.87 us (13%)
  local copies, waits for them, and re-layouts  1.62 us (3%)
  between operations  0.79 us (1%)
    ppermute x21, starting transfers between devices, swap(): lax.ppermute(value, axis, [(j, j ^ k) for j in range(lax.axis_size(axis))])  34.4 us
    pallas_call x5, Pallas kernels, call(): pl.pallas_call(kernel, in_specs=in_specs or [vmem] * len(operands), out_s...  9.66 us
    ppermute x21, waiting for transfers between devices, swap(): lax.ppermute(value, axis, [(j, j ^ k) for j in range(lax.axis_size(axis))])  6.87 us
    unnamed x16, local copies, waits for them, and re-layouts  1.62 us
  transfers between devices with their start and end apart: 21, of which 4 were waited for; matrix products, arithmetic and copies ran while one was open for 1% of the time, Pallas kernels for 12%

commit v1 on v0

--- a/solution.py
+++ b/solution.py
@@ -47,54 +47,47 @@
     )(*operands))
 
 
-def product_kernel(axis, near, far, *refs):
-    in_refs, out_refs = refs[:4], refs[4:-2]
+def product_kernel(axis, plan, *refs):
+    count = 2 * (1 + max(pair for _, pair, _ in plan))
+    in_refs, out_refs = refs[:count], refs[count:-2]
     buf_ref, sems = refs[-2:]
-    both_refs = dict(zip(near, out_refs))
-    gated_refs = dict(zip(far, out_refs[len(near) :]))
-    saved_refs = dict(zip(far, out_refs[len(near) + len(far) :]))
     rows = buf_ref.shape[2]
-    copies = {}
-    for k in far + near:
-        copies[k] = [
-            pltpu.make_async_copy(
-                in_ref.at[peer_rows(axis, k, rows)], buf_ref.at[j, k], sems.at[j, k]
-            )
-            for j, in_ref in enumerate(in_refs)
-        ]
-        for copy in copies[k]:
+    copies = []
+    for i, (k, pair, _) in enumerate(plan):
+        copies.append(
+            [
+                pltpu.make_async_copy(
+                    in_refs[2 * pair + j].at[peer_rows(axis, k, rows)], buf_ref.at[j, i], sems.at[j, i]
+                )
+                for j in range(2)
+            ]
+        )
+        for copy in copies[i]:
             copy.start()
-    for k in far + near:
-        for copy in copies[k]:
+    for i, (_, _, (at, slot)) in enumerate(plan):
+        for copy in copies[i]:
             copy.wait()
-        gated = (buf_ref[0, k].astype(f32) * buf_ref[1, k].astype(f32)).astype(bf16)
-        saved = (buf_ref[2, k].astype(f32) * buf_ref[3, k].astype(f32)).astype(bf16)
-        if k in both_refs:
-            both_refs[k][0] = gated
-            both_refs[k][1] = saved
+        value = (buf_ref[0, i].astype(f32) * buf_ref[1, i].astype(f32)).astype(bf16)
+        if slot is None:
+            out_refs[at][...] = value
         else:
-            gated_refs[k][...] = gated
-            saved_refs[k][...] = saved
-
-
-def product(arrays, near, far, axis):
-    count = len(near) + len(far)
+            out_refs[at][slot] = value
+
+
+def product(arrays, plan, slots, count, axis):
     channels, block = arrays[0].shape
     rows = channels // count
-    out = call(
-        functools.partial(product_kernel, axis, near, far),
+    return call(
+        functools.partial(product_kernel, axis, plan),
         None,
-        [jax.ShapeDtypeStruct((2, rows, block), bf16)] * len(near)
-        + [jax.ShapeDtypeStruct((rows, block), bf16)] * (2 * len(far)),
-        [pltpu.VMEM((4, count, rows, block), bf16), pltpu.SemaphoreType.DMA((4, count))],
-        2 * channels * block,
-        12 * channels * block,
+        [jax.ShapeDtypeStruct(((n,) if n > 1 else ()) + (rows, block), bf16) for n in slots],
+        [pltpu.VMEM((2, len(plan), rows, block), bf16), pltpu.SemaphoreType.DMA((2, len(plan)))],
+        len(plan) * rows * block,
+        6 * len(plan) * rows * block,
         4,
         in_hbm(*arrays),
-        [pl.BlockSpec(memory_space=pltpu.HBM)] * 4,
-    )
-    ends = [len(near), count, count + len(far)]
-    return [dict(zip(ks, out[lo:hi])) for ks, lo, hi in zip((near, far, far), [0] + ends, ends)]
+        [pl.BlockSpec(memory_space=pltpu.HBM)] * len(arrays),
+    )
 
 
 def filter_kernel(filt_ref, low_ref, high_ref, spec_ref):
@@ -322,10 +315,15 @@
     token_count = seqs * shares * length
     near, far = peers(groups)
     rows = [x.reshape(channels, block) for x in (grad_output, post_gate, pre_gate, value_branch)]
-    both, gated, saved = product(rows, near, far, "ctx")
-    gated = [swap(gated[k], "ctx", k) for k in far]
-    both = [both[0]] + [swap(both[k], "ctx", k) for k in near[1:]]
-    saved = [swap(saved[k], "ctx", k) for k in far]
+    first = [(k, 0, (i, None)) for i, k in enumerate(far)]
+    gated = product(rows[:2], first, [1] * len(far), groups, "ctx")
+    gated = [swap(value, "ctx", k) for k, value in zip(far, gated)]
+    rest = [(k, pair, (i, pair)) for i, k in enumerate(near[1:] + near[:1]) for pair in range(2)]
+    rest += [(k, 1, (len(near) + i, None)) for i, k in enumerate(far)]
+    out = product(rows, rest, [2] * len(near) + [1] * len(far), groups, "ctx")
+    saved = [swap(value, "ctx", k) for k, value in zip(far, out[len(near) :])]
+    both = [swap(value, "ctx", k) for k, value in zip(near[1:], out)]
+    both = [out[len(near) - 1]] + both
     w, filt_spec = filter_spectrum_dense(long_filter)
     own = (rows[0].astype(f32) * rows[1].astype(f32)).astype(bf16)
     base = skip_weight[:, None] * own.astype(f32)

time: 53.8 us -> 53.3 us (level)
  waiting for transfers between devices: 6.87 us -> 9.65 us
  starting transfers between devices: 34.4 us -> 31.7 us
  local copies, waits for them, and re-layouts: 1.62 us -> 0.03 us
  Pallas kernels: 9.66 us -> 10.6 us
    ppermute x21, waiting for transfers between devices: 6.87 us -> 9.65 us  [swap(): lax.ppermute(value, axis, [(j, j ^ k) for j in range(lax.axis_size(axis))])]
    ppermute x21, starting transfers between devices: 34.4 us -> 31.7 us  [swap(): lax.ppermute(value, axis, [(j, j ^ k) for j in range(lax.axis_size(axis))])]
    unnamed x16 -> x14, local copies, waits for them, and re-layouts: 1.62 us -> 0.03 us
    pallas_call x5 -> x6, Pallas kernels: 9.66 us -> 10.6 us  [call(): pl.pallas_call(kernel, in_specs=in_specs or [vmem] * len(operands), out_s...]
  transfers between devices with their start and end apart: 21 -> 21, of which waited for: 4 -> 5; matrix products, arithmetic and copies ran while one was open for 1% -> 1% of each run, Pallas kernels for 12% -> 15%
where the time goes in v1:
time: 53.3 us; the launch traced here: 53.1 us
  starting transfers between devices  31.7 us (59%)
  Pallas kernels  10.6 us (20%)
  waiting for transfers between devices  9.65 us (18%)
  between operations  0.79 us (1%)
    ppermute x21, starting transfers between devices, swap(): lax.ppermute(value, axis, [(j, j ^ k) for j in range(lax.axis_size(axis))])  31.7 us
    pallas_call x6, Pallas kernels, call(): pl.pallas_call(kernel, in_specs=in_specs or [vmem] * len(operands), out_s...  10.6 us
    ppermute x21, waiting for transfers between devices, swap(): lax.ppermute(value, axis, [(j, j ^ k) for j in range(lax.axis_size(axis))])  9.65 us
  transfers between devices with their start and end apart: 21, of which 5 were waited for; matrix products, arithmetic and copies ran while one was open for 1% of the time, Pallas kernels for 15%

profile of v1, /device:TPU:0, one launch (start us, length us, event | category | flops | bytes accessed | tf_op | source)
XLA Modules:
  0.0 53.1 jit_solution(5766338043654864818)
XLA Ops:
  0.6 0.0 copy-start.3
  0.7 1.3 %shard_map.96 = (bf16[256,128]{1,0:T(8,128)(2,1)S(1)}, bf16[256,128]{1,0:T(8,128)(2,1)S(1)}, bf16[256,128]{1,0:T(8,128)(2,1)S(1)}, bf16[256,128]{1,0:T(8,128)(2,1)S(1)}) custom-call(bf16[2048,128]{1,0:T(8,128)(2,1)} %bitcast.14, bf16[2048,128]{1,0:T(8,128)(2,1)} %bitcast.12), custom_call_target="tpu_custom_call" | custom-call | flops 131072 | bytes 786432 | tf_op jit(solution)/shard_map/pallas_call | solution.py:39
  2.0 4.1 %collective-permute-start.3 = (bf16[256,128]{1,0:T(8,128)(2,1)S(1)}, bf16[256,128]{1,0:T(8,128)(2,1)S(1)}, u32[]{:S(2)}, u32[]{:S(2)}) collective-permute-start(bf16[256,128]{1,0:T(8,128)(2,1)S(1)} %get-tuple-element.39), channel_id=1, source_target_pairs={{0,4},{1,5},{2,6},{3,7},{4,0},{5,1},{6,2},{7,3},{8,12},{9,13},{10,... | collective-permute-start | bytes 196616 | tf_op jit(solution)/shard_map/ppermute | solution.py:303
  6.1 1.3 %collective-permute-start.4 = (bf16[256,128]{1,0:T(8,128)(2,1)S(1)}, bf16[256,128]{1,0:T(8,128)(2,1)S(1)}, u32[]{:S(2)}, u32[]{:S(2)}) collective-permute-start(bf16[256,128]{1,0:T(8,128)(2,1)S(1)} %get-tuple-element.40), channel_id=1, source_target_pairs={{0,5},{1,4},{2,7},{3,6},{4,1},{5,0},{6,3},{7,2},{8,13},{9,12},{10,... | collective-permute-start | bytes 196616 | tf_op jit(solution)/shard_map/ppermute | solution.py:303
  7.4 1.6 %shard_map.95 = (bf16[2,256,128]{2,1,0:T(8,128)(2,1)S(1)}, bf16[2,256,128]{2,1,0:T(8,128)(2,1)S(1)}, bf16[2,256,128]{2,1,0:T(8,128)(2,1)S(1)}, bf16[2,256,128]{2...) custom-call(bf16[2048,128]{1,0:T(8,128)(2,1)} %bitcast.15, ...), custom_call_target="tpu_custom_call" | custom-call | flops 393216 | bytes 2359296 | tf_op jit(solution)/shard_map/pallas_call | solution.py:39
  9.0 0.3 collective-permute-start
  9.3 1.8 %collective-permute-start.1 = (bf16[2,256,128]{2,1,0:T(8,128)(2,1)S(1)}, bf16[2,256,128]{2,1,0:T(8,128)(2,1)S(1)}, u32[]{:S(2)}, u32[]{:S(2)}) collective-permute-start(bf16[2,256,128]{2,1,0:T(8,128)(2,1)S(1)} %get-tuple-element.37), channel_id=1, source_target_pairs={{0,2},{1,3},{2,0},{3,1},{4,6},{5,7},{6,4},{7,5},{8,10},{9,11},{10,... | collective-permute-start | bytes 393224 | tf_op jit(solution)/shard_map/ppermute | solution.py:303
  11.2 1.4 %collective-permute-start.2 = (bf16[2,256,128]{2,1,0:T(8,128)(2,1)S(1)}, bf16[2,256,128]{2,1,0:T(8,128)(2,1)S(1)}, u32[]{:S(2)}, u32[]{:S(2)}) collective-permute-start(bf16[2,256,128]{2,1,0:T(8,128)(2,1)S(1)} %get-tuple-element.38), channel_id=1, source_target_pairs={{0,3},{1,2},{2,1},{3,0},{4,7},{5,6},{6,5},{7,4},{8,11},{9,10},{10,... | collective-permute-start | bytes 393224 | tf_op jit(solution)/shard_map/ppermute | solution.py:303
  12.6 0.0 collective-permute-done.3.refs_4_
  12.6 3.6 %collective-permute-start.5 = (bf16[256,128]{1,0:T(8,128)(2,1)S(1)}, bf16[256,128]{1,0:T(8,128)(2,1)S(1)}, u32[]{:S(2)}, u32[]{:S(2)}) collective-permute-start(bf16[256,128]{1,0:T(8,128)(2,1)S(1)} %get-tuple-element.41), channel_id=1, source_target_pairs={{0,6},{1,7},{2,4},{3,5},{4,2},{5,3},{6,0},{7,1},{8,14},{9,15},{10,... | collective-permute-start | bytes 196616 | tf_op jit(solution)/shard_map/ppermute | solution.py:303
  16.2 0.0 collective-permute-done.4.refs_5_
  16.2 0.8 %collective-permute-start.6 = (bf16[256,128]{1,0:T(8,128)(2,1)S(1)}, bf16[256,128]{1,0:T(8,128)(2,1)S(1)}, u32[]{:S(2)}, u32[]{:S(2)}) collective-permute-start(bf16[256,128]{1,0:T(8,128)(2,1)S(1)} %get-tuple-element.42), channel_id=1, source_target_pairs={{0,7},{1,6},{2,5},{3,4},{4,3},{5,2},{6,1},{7,0},{8,15},{9,14},{10,... | collective-permute-start | bytes 196616 | tf_op jit(solution)/shard_map/ppermute | solution.py:303
  17.0 1.4 %shard_map.94 = (bf16[512,2048]{1,0:T(8,128)(2,1)S(1)}, f32[256,2048]{1,0:T(8,128)S(1)}) custom-call(f32[256,1024]{1,0:T(8,128)S(1)} %copy-done.2, bf16[512,2048]{1,0:T(8,128)(2,1)S(1)} %copy-done.3), custom_call_target="tpu_custom_call" | custom-call | flops 1073741824 | bytes 7340032 | tf_op jit(solution)/shard_map/pallas_call | solution.py:39
  18.4 3.5 %collective-permute-done.5.refs_6_ = bf16[256,128]{1,0:T(8,128)(2,1)S(1)} collective-permute-done((bf16[256,128]{1,0:T(8,128)(2,1)S(1)}, bf16[256,128]{1,0:T(8,128)(2,1)S(1)}, u32[]{:S(2)}, u32[]{:S(2)}) %collective-permute-start.5) | collective-permute-done | bytes 65568 | tf_op jit(solution)/shard_map/ppermute | solution.py:303
  21.9 0.0 collective-permute-start.14
  21.9 1.6 %collective-permute-done.6.refs_7_ = bf16[256,128]{1,0:T(8,128)(2,1)S(1)} collective-permute-done((bf16[256,128]{1,0:T(8,128)(2,1)S(1)}, bf16[256,128]{1,0:T(8,128)(2,1)S(1)}, u32[]{:S(2)}, u32[]{:S(2)}) %collective-permute-start.6) | collective-permute-done | bytes 65568 | tf_op jit(solution)/shard_map/ppermute | solution.py:303
  23.5 1.3 %collective-permute-start.15 = (bf16[256,128]{1,0:T(8,128)(2,1)S(1)}, bf16[256,128]{1,0:T(8,128)(2,1)S(1)}, u32[]{:S(2)}, u32[]{:S(2)}) collective-permute-start(bf16[256,128]{1,0:T(8,128)(2,1)S(1)} %get-tuple-element.53), channel_id=1, source_target_pairs={{0,5},{1,4},{2,7},{3,6},{4,1},{5,0},{6,3},{7,2},{8,13},{9,12},{10,... | collective-permute-start | bytes 196616 | tf_op jit(solution)/shard_map/ppermute | solution.py:303
  24.8 0.0 collective-permute-done.refs_1_
  24.8 1.1 %collective-permute-start.16 = (bf16[256,128]{1,0:T(8,128)(2,1)S(1)}, bf16[256,128]{1,0:T(8,128)(2,1)S(1)}, u32[]{:S(2)}, u32[]{:S(2)}) collective-permute-start(bf16[256,128]{1,0:T(8,128)(2,1)S(1)} %get-tuple-element.54), channel_id=1, source_target_pairs={{0,6},{1,7},{2,4},{3,5},{4,2},{5,3},{6,0},{7,1},{8,14},{9,15},{10,... | collective-permute-start | bytes 196616 | tf_op jit(solution)/shard_map/ppermute | solution.py:303
  25.9 0.0 collective-permute-done.1.refs_2_
  25.9 3.6 %collective-permute-start.17 = (bf16[256,128]{1,0:T(8,128)(2,1)S(1)}, bf16[256,128]{1,0:T(8,128)(2,1)S(1)}, u32[]{:S(2)}, u32[]{:S(2)}) collective-permute-start(bf16[256,128]{1,0:T(8,128)(2,1)S(1)} %get-tuple-element.55), channel_id=1, source_target_pairs={{0,7},{1,6},{2,5},{3,4},{4,3},{5,2},{6,1},{7,0},{8,15},{9,14},{10,... | collective-permute-start | bytes 196616 | tf_op jit(solution)/shard_map/ppermute | solution.py:303
  29.5 0.0 collective-permute-done.2.refs_3_
  29.5 2.5 %shard_map.97 = (bf16[256,128]{1,0:T(8,128)(2,1)S(1)}, bf16[256,128]{1,0:T(8,128)(2,1)S(1)}, bf16[256,128]{1,0:T(8,128)(2,1)S(1)}, bf16[256,128]{1,0:T(8,128)(2,...) custom-call(bf16[512,2048]{1,0:T(8,128)(2,1)S(1)} %copy-done.3, ...), custom_call_target="tpu_custom_call" | custom-call | flops 2147483648 | bytes 9437184 | tf_op jit(solution)/shard_map/pallas_call | solution.py:39
  32.0 0.1 collective-permute-start.10
  32.1 2.9 %collective-permute-start.11 = (bf16[256,128]{1,0:T(8,128)(2,1)S(1)}, bf16[256,128]{1,0:T(8,128)(2,1)S(1)}, u32[]{:S(2)}, u32[]{:S(2)}) collective-permute-start(bf16[256,128]{1,0:T(8,128)(2,1)S(1)} %get-tuple-element.48), channel_id=1, source_target_pairs={{0,5},{1,4},{2,7},{3,6},{4,1},{5,0},{6,3},{7,2},{8,13},{9,12},{10,... | collective-permute-start | bytes 196616 | tf_op jit(solution)/shard_map/ppermute | solution.py:303
  35.0 0.0 collective-permute-done.15.refs_5_
  35.0 1.1 %collective-permute-start.12 = (bf16[256,128]{1,0:T(8,128)(2,1)S(1)}, bf16[256,128]{1,0:T(8,128)(2,1)S(1)}, u32[]{:S(2)}, u32[]{:S(2)}) collective-permute-start(bf16[256,128]{1,0:T(8,128)(2,1)S(1)} %get-tuple-element.49), channel_id=1, source_target_pairs={{0,6},{1,7},{2,4},{3,5},{4,2},{5,3},{6,0},{7,1},{8,14},{9,15},{10,... | collective-permute-start | bytes 196616 | tf_op jit(solution)/shard_map/ppermute | solution.py:303
  36.2 0.0 collective-permute-done.16.refs_6_
  36.2 3.6 %collective-permute-start.13 = (bf16[256,128]{1,0:T(8,128)(2,1)S(1)}, bf16[256,128]{1,0:T(8,128)(2,1)S(1)}, u32[]{:S(2)}, u32[]{:S(2)}) collective-permute-start(bf16[256,128]{1,0:T(8,128)(2,1)S(1)} %get-tuple-element.50), channel_id=1, source_target_pairs={{0,7},{1,6},{2,5},{3,4},{4,3},{5,2},{6,1},{7,0},{8,15},{9,14},{10,... | collective-permute-start | bytes 196616 | tf_op jit(solution)/shard_map/ppermute | solution.py:303
  39.8 0.0 collective-permute-done.17.refs_7_
  39.8 0.6 %collective-permute-start.7 = (bf16[256,128]{1,0:T(8,128)(2,1)S(1)}, bf16[256,128]{1,0:T(8,128)(2,1)S(1)}, u32[]{:S(2)}, u32[]{:S(2)}) collective-permute-start(bf16[256,128]{1,0:T(8,128)(2,1)S(1)} %get-tuple-element.44), channel_id=1, source_target_pairs={{0,1},{1,0},{2,3},{3,2},{4,5},{5,4},{6,7},{7,6},{8,9},{9,8},{10,11... | collective-permute-start | bytes 196616 | tf_op jit(solution)/shard_map/ppermute | solution.py:303
  40.3 2.5 %shard_map.98 = (bf16[256,256]{1,0:T(8,128)(2,1)S(1)}, bf16[256,256]{1,0:T(8,128)(2,1)S(1)}, bf16[256,256]{1,0:T(8,128)(2,1)S(1)}, bf16[256,256]{1,0:T(8,128)(2,1)S(1)}) custom-call(bf16[512,2048]{1,0:T(8,128)(2,1)S(1)} %copy-done.3, bf16[512,2048]{1,0:T(8,128)(2,1)S(1)} %get-tuple-element.33.high_ref, f32[256,2048]{1,0:T(8,128)S(1)} %get-tuple-element.51.grad_spec_ref, ...), custom_call_target="tpu_custom_call" | custom-call | flops 2147483648 | bytes 9437184 | tf_op jit(solution)/shard_map/pallas_call | solution.py:39
  42.9 0.0 copy-start
  42.9 0.0 copy-start.1
  42.9 0.1 collective-permute-start.18
  43.0 0.9 %collective-permute-done.11.refs_5_ = bf16[256,128]{1,0:T(8,128)(2,1)S(1)} collective-permute-done((bf16[256,128]{1,0:T(8,128)(2,1)S(1)}, bf16[256,128]{1,0:T(8,128)(2,1)S(1)}, u32[]{:S(2)}, u32[]{:S(2)}) %collective-permute-start.11) | collective-permute-done | bytes 65568 | tf_op jit(solution)/shard_map/ppermute | solution.py:303
  43.9 1.5 %collective-permute-start.19 = (bf16[256,256]{1,0:T(8,128)(2,1)S(1)}, bf16[256,256]{1,0:T(8,128)(2,1)S(1)}, u32[]{:S(2)}, u32[]{:S(2)}) collective-permute-start(bf16[256,256]{1,0:T(8,128)(2,1)S(1)} %get-tuple-element.58), channel_id=1, source_target_pairs={{0,16},{8,24},{16,0},{24,8},{1,17},{9,25},{17,1},{25,9},{2,18},{10... | collective-permute-start | bytes 393224 | tf_op jit(solution)/shard_map/ppermute | solution.py:303
  45.4 0.0 collective-permute-start.20
  45.4 0.0 collective-permute-done.13.refs_7_
  45.4 0.6 %collective-permute-start.8 = (bf16[256,128]{1,0:T(8,128)(2,1)S(1)}, bf16[256,128]{1,0:T(8,128)(2,1)S(1)}, u32[]{:S(2)}, u32[]{:S(2)}) collective-permute-start(bf16[256,128]{1,0:T(8,128)(2,1)S(1)} %get-tuple-element.45), channel_id=1, source_target_pairs={{0,2},{1,3},{2,0},{3,1},{4,6},{5,7},{6,4},{7,5},{8,10},{9,11},{10,... | collective-permute-start | bytes 196616 | tf_op jit(solution)/shard_map/ppermute | solution.py:303
  46.0 0.0 collective-permute-done.7.refs_1_
  46.0 1.8 %collective-permute-start.9 = (bf16[256,128]{1,0:T(8,128)(2,1)S(1)}, bf16[256,128]{1,0:T(8,128)(2,1)S(1)}, u32[]{:S(2)}, u32[]{:S(2)}) collective-permute-start(bf16[256,128]{1,0:T(8,128)(2,1)S(1)} %get-tuple-element.46), channel_id=1, source_target_pairs={{0,3},{1,2},{2,1},{3,0},{4,7},{5,6},{6,5},{7,4},{8,11},{9,10},{10,... | collective-permute-start | bytes 196616 | tf_op jit(solution)/shard_map/ppermute | solution.py:303
  47.8 0.3 convert_multiply_fusion.base_ref
  48.2 2.2 %collective-permute-done.8.refs_2_ = bf16[256,128]{1,0:T(8,128)(2,1)S(1)} collective-permute-done((bf16[256,128]{1,0:T(8,128)(2,1)S(1)}, bf16[256,128]{1,0:T(8,128)(2,1)S(1)}, u32[]{:S(2)}, u32[]{:S(2)}) %collective-permute-start.8) | collective-permute-done | bytes 65568 | tf_op jit(solution)/shard_map/ppermute | solution.py:303
  50.4 1.4 %collective-permute-done.9.refs_3_ = bf16[256,128]{1,0:T(8,128)(2,1)S(1)} collective-permute-done((bf16[256,128]{1,0:T(8,128)(2,1)S(1)}, bf16[256,128]{1,0:T(8,128)(2,1)S(1)}, u32[]{:S(2)}, u32[]{:S(2)}) %collective-permute-start.9) | collective-permute-done | bytes 65568 | tf_op jit(solution)/shard_map/ppermute | solution.py:303
  51.8 0.0 collective-permute-done.19.refs_10_
  51.8 0.0 collective-permute-done.20.refs_11_
  51.8 1.3 %shard_map.99 = (bf16[2048,128]{1,0:T(8,128)(2,1)}, bf16[2048,128]{1,0:T(8,128)(2,1)}, f32[256,256]{1,0:T(8,128)}) custom-call(f32[2048,128]{1,0:T(8,128)S(1)} %convert_multiply_fusion.base_ref, bf16[2048,128]{1,0:T(8,128)(2,1)S(1)} %bitcast.9, bf16[2048,128]{1,0:T(8,128)(2,1)S(1)} %bitcast.11, bf16[256,128]{1,0:T(8,128)(2,1)S(1)} %get-tuple-element.43.refs_0_, ...), custom_call_target="tpu_custom_call" | custom-call | flops 786432 | bytes 3670016 | tf_op jit(solution)/shard_map/pallas_call | solution.py:39
  (15 shorter events, 0.0 us)
Async XLA Ops:
  0.6 16.3 %copy-start.3 = (bf16[512,2048]{1,0:T(8,128)(2,1)S(1)}, bf16[512,2048]{1,0:T(8,128)(2,1)}, u32[]{:S(2)}) copy-start(bf16[512,2048]{1,0:T(8,128)(2,1)} %constant.2.clone.low_ref) | copy-start | bytes 6291460
  0.6 16.3 %copy-start.2 = (f32[256,1024]{1,0:T(8,128)S(1)}, f32[256,1024]{1,0:T(8,128)}, u32[]{:S(2)}) copy-start(f32[256,1024]{1,0:T(8,128)} %filt_ref.1) | copy-start | bytes 3145732
  2.0 10.6 %collective-permute-start.3 = (bf16[256,128]{1,0:T(8,128)(2,1)S(1)}, bf16[256,128]{1,0:T(8,128)(2,1)S(1)}, u32[]{:S(2)}, u32[]{:S(2)}) collective-permute-start(bf16[256,128]{1,0:T(8,128)(2,1)S(1)} %get-tuple-element.39), channel_id=1, source_target_pairs={{0,4},{1,5},{2,6},{3,7},{4,0},{5,1},{6,2},{7,3},{8,12},{9,13},{10,... | collective-permute-start | bytes 196616 | tf_op jit(solution)/shard_map/ppermute | solution.py:303
  6.1 10.1 %collective-permute-start.4 = (bf16[256,128]{1,0:T(8,128)(2,1)S(1)}, bf16[256,128]{1,0:T(8,128)(2,1)S(1)}, u32[]{:S(2)}, u32[]{:S(2)}) collective-permute-start(bf16[256,128]{1,0:T(8,128)(2,1)S(1)} %get-tuple-element.40), channel_id=1, source_target_pairs={{0,5},{1,4},{2,7},{3,6},{4,1},{5,0},{6,3},{7,2},{8,13},{9,12},{10,... | collective-permute-start | bytes 196616 | tf_op jit(solution)/shard_map/ppermute | solution.py:303
  9.0 15.8 %collective-permute-start = (bf16[2,256,128]{2,1,0:T(8,128)(2,1)S(1)}, bf16[2,256,128]{2,1,0:T(8,128)(2,1)S(1)}, u32[]{:S(2)}, u32[]{:S(2)}) collective-permute-start(bf16[2,256,128]{2,1,0:T(8,128)(2,1)S(1)} %get-tuple-element.36), channel_id=1, source_target_pairs={{0,1},{1,0},{2,3},{3,2},{4,5},{5,4},{6,7},{7,6},{8,9},{9,8},{10,11... | collective-permute-start | bytes 393224 | tf_op jit(solution)/shard_map/ppermute | solution.py:303
  9.3 16.6 %collective-permute-start.1 = (bf16[2,256,128]{2,1,0:T(8,128)(2,1)S(1)}, bf16[2,256,128]{2,1,0:T(8,128)(2,1)S(1)}, u32[]{:S(2)}, u32[]{:S(2)}) collective-permute-start(bf16[2,256,128]{2,1,0:T(8,128)(2,1)S(1)} %get-tuple-element.37), channel_id=1, source_target_pairs={{0,2},{1,3},{2,0},{3,1},{4,6},{5,7},{6,4},{7,5},{8,10},{9,11},{10,... | collective-permute-start | bytes 393224 | tf_op jit(solution)/shard_map/ppermute | solution.py:303
  11.2 18.4 %collective-permute-start.2 = (bf16[2,256,128]{2,1,0:T(8,128)(2,1)S(1)}, bf16[2,256,128]{2,1,0:T(8,128)(2,1)S(1)}, u32[]{:S(2)}, u32[]{:S(2)}) collective-permute-start(bf16[2,256,128]{2,1,0:T(8,128)(2,1)S(1)} %get-tuple-element.38), channel_id=1, source_target_pairs={{0,3},{1,2},{2,1},{3,0},{4,7},{5,6},{6,5},{7,4},{8,11},{9,10},{10,... | collective-permute-start | bytes 393224 | tf_op jit(solution)/shard_map/ppermute | solution.py:303
  12.6 9.3 %collective-permute-start.5 = (bf16[256,128]{1,0:T(8,128)(2,1)S(1)}, bf16[256,128]{1,0:T(8,128)(2,1)S(1)}, u32[]{:S(2)}, u32[]{:S(2)}) collective-permute-start(bf16[256,128]{1,0:T(8,128)(2,1)S(1)} %get-tuple-element.41), channel_id=1, source_target_pairs={{0,6},{1,7},{2,4},{3,5},{4,2},{5,3},{6,0},{7,1},{8,14},{9,15},{10,... | collective-permute-start | bytes 196616 | tf_op jit(solution)/shard_map/ppermute | solution.py:303
  16.2 7.3 %collective-permute-start.6 = (bf16[256,128]{1,0:T(8,128)(2,1)S(1)}, bf16[256,128]{1,0:T(8,128)(2,1)S(1)}, u32[]{:S(2)}, u32[]{:S(2)}) collective-permute-start(bf16[256,128]{1,0:T(8,128)(2,1)S(1)} %get-tuple-element.42), channel_id=1, source_target_pairs={{0,7},{1,6},{2,5},{3,4},{4,3},{5,2},{6,1},{7,0},{8,15},{9,14},{10,... | collective-permute-start | bytes 196616 | tf_op jit(solution)/shard_map/ppermute | solution.py:303
  21.9 10.2 %collective-permute-start.14 = (bf16[256,128]{1,0:T(8,128)(2,1)S(1)}, bf16[256,128]{1,0:T(8,128)(2,1)S(1)}, u32[]{:S(2)}, u32[]{:S(2)}) collective-permute-start(bf16[256,128]{1,0:T(8,128)(2,1)S(1)} %get-tuple-element.52), channel_id=1, source_target_pairs={{0,4},{1,5},{2,6},{3,7},{4,0},{5,1},{6,2},{7,3},{8,12},{9,13},{10,... | collective-permute-start | bytes 196616 | tf_op jit(solution)/shard_map/ppermute | solution.py:303
  23.5 11.6 %collective-permute-start.15 = (bf16[256,128]{1,0:T(8,128)(2,1)S(1)}, bf16[256,128]{1,0:T(8,128)(2,1)S(1)}, u32[]{:S(2)}, u32[]{:S(2)}) collective-permute-start(bf16[256,128]{1,0:T(8,128)(2,1)S(1)} %get-tuple-element.53), channel_id=1, source_target_pairs={{0,5},{1,4},{2,7},{3,6},{4,1},{5,0},{6,3},{7,2},{8,13},{9,12},{10,... | collective-permute-start | bytes 196616 | tf_op jit(solution)/shard_map/ppermute | solution.py:303
  24.8 11.3 %collective-permute-start.16 = (bf16[256,128]{1,0:T(8,128)(2,1)S(1)}, bf16[256,128]{1,0:T(8,128)(2,1)S(1)}, u32[]{:S(2)}, u32[]{:S(2)}) collective-permute-start(bf16[256,128]{1,0:T(8,128)(2,1)S(1)} %get-tuple-element.54), channel_id=1, source_target_pairs={{0,6},{1,7},{2,4},{3,5},{4,2},{5,3},{6,0},{7,1},{8,14},{9,15},{10,... | collective-permute-start | bytes 196616 | tf_op jit(solution)/shard_map/ppermute | solution.py:303
  25.9 13.8 %collective-permute-start.17 = (bf16[256,128]{1,0:T(8,128)(2,1)S(1)}, bf16[256,128]{1,0:T(8,128)(2,1)S(1)}, u32[]{:S(2)}, u32[]{:S(2)}) collective-permute-start(bf16[256,128]{1,0:T(8,128)(2,1)S(1)} %get-tuple-element.55), channel_id=1, source_target_pairs={{0,7},{1,6},{2,5},{3,4},{4,3},{5,2},{6,1},{7,0},{8,15},{9,14},{10,... | collective-permute-start | bytes 196616 | tf_op jit(solution)/shard_map/ppermute | solution.py:303
  32.0 10.9 %collective-permute-start.10 = (bf16[256,128]{1,0:T(8,128)(2,1)S(1)}, bf16[256,128]{1,0:T(8,128)(2,1)S(1)}, u32[]{:S(2)}, u32[]{:S(2)}) collective-permute-start(bf16[256,128]{1,0:T(8,128)(2,1)S(1)} %get-tuple-element.47), channel_id=1, source_target_pairs={{0,4},{1,5},{2,6},{3,7},{4,0},{5,1},{6,2},{7,3},{8,12},{9,13},{10,... | collective-permute-start | bytes 196616 | tf_op jit(solution)/shard_map/ppermute | solution.py:303
  32.1 11.8 %collective-permute-start.11 = (bf16[256,128]{1,0:T(8,128)(2,1)S(1)}, bf16[256,128]{1,0:T(8,128)(2,1)S(1)}, u32[]{:S(2)}, u32[]{:S(2)}) collective-permute-start(bf16[256,128]{1,0:T(8,128)(2,1)S(1)} %get-tuple-element.48), channel_id=1, source_target_pairs={{0,5},{1,4},{2,7},{3,6},{4,1},{5,0},{6,3},{7,2},{8,13},{9,12},{10,... | collective-permute-start | bytes 196616 | tf_op jit(solution)/shard_map/ppermute | solution.py:303
  35.0 10.4 %collective-permute-start.12 = (bf16[256,128]{1,0:T(8,128)(2,1)S(1)}, bf16[256,128]{1,0:T(8,128)(2,1)S(1)}, u32[]{:S(2)}, u32[]{:S(2)}) collective-permute-start(bf16[256,128]{1,0:T(8,128)(2,1)S(1)} %get-tuple-element.49), channel_id=1, source_target_pairs={{0,6},{1,7},{2,4},{3,5},{4,2},{5,3},{6,0},{7,1},{8,14},{9,15},{10,... | collective-permute-start | bytes 196616 | tf_op jit(solution)/shard_map/ppermute | solution.py:303
  36.2 9.2 %collective-permute-start.13 = (bf16[256,128]{1,0:T(8,128)(2,1)S(1)}, bf16[256,128]{1,0:T(8,128)(2,1)S(1)}, u32[]{:S(2)}, u32[]{:S(2)}) collective-permute-start(bf16[256,128]{1,0:T(8,128)(2,1)S(1)} %get-tuple-element.50), channel_id=1, source_target_pairs={{0,7},{1,6},{2,5},{3,4},{4,3},{5,2},{6,1},{7,0},{8,15},{9,14},{10,... | collective-permute-start | bytes 196616 | tf_op jit(solution)/shard_map/ppermute | solution.py:303
  39.8 6.3 %collective-permute-start.7 = (bf16[256,128]{1,0:T(8,128)(2,1)S(1)}, bf16[256,128]{1,0:T(8,128)(2,1)S(1)}, u32[]{:S(2)}, u32[]{:S(2)}) collective-permute-start(bf16[256,128]{1,0:T(8,128)(2,1)S(1)} %get-tuple-element.44), channel_id=1, source_target_pairs={{0,1},{1,0},{2,3},{3,2},{4,5},{5,4},{6,7},{7,6},{8,9},{9,8},{10,11... | collective-permute-start | bytes 196616 | tf_op jit(solution)/shard_map/ppermute | solution.py:303
  40.3 7.5 %copy-start.4 = (bf16[1,2048,128]{2,1,0:T(8,128)(2,1)S(1)}, bf16[1,2048,128]{2,1,0:T(8,128)(2,1)}, u32[]{:S(2)}) copy-start(bf16[1,2048,128]{2,1,0:T(8,128)(2,1)} %param.8) | copy-start | bytes 1572868
  40.3 7.5 %copy-start.5 = (bf16[1,2048,128]{2,1,0:T(8,128)(2,1)S(1)}, bf16[1,2048,128]{2,1,0:T(8,128)(2,1)}, u32[]{:S(2)}) copy-start(bf16[1,2048,128]{2,1,0:T(8,128)(2,1)} %param.7) | copy-start | bytes 1572868
  40.3 7.5 %copy-start.6 = (f32[2048]{0:T(1024)S(1)}, f32[2048]{0:T(1024)}, u32[]{:S(2)}) copy-start(f32[2048]{0:T(1024)} %param.12) | copy-start | bytes 24580
  42.9 8.9 %copy-start = (bf16[1,2048,128]{2,1,0:T(8,128)(2,1)S(1)}, bf16[1,2048,128]{2,1,0:T(8,128)(2,1)}, u32[]{:S(2)}) copy-start(bf16[1,2048,128]{2,1,0:T(8,128)(2,1)} %param.9) | copy-start | bytes 1572868
  42.9 8.9 %copy-start.1 = (bf16[1,2048,128]{2,1,0:T(8,128)(2,1)S(1)}, bf16[1,2048,128]{2,1,0:T(8,128)(2,1)}, u32[]{:S(2)}) copy-start(bf16[1,2048,128]{2,1,0:T(8,128)(2,1)} %param.10) | copy-start | bytes 1572868
  42.9 8.9 %collective-permute-start.18 = (bf16[256,256]{1,0:T(8,128)(2,1)S(1)}, bf16[256,256]{1,0:T(8,128)(2,1)S(1)}, u32[]{:S(2)}, u32[]{:S(2)}) collective-permute-start(bf16[256,256]{1,0:T(8,128)(2,1)S(1)} %get-tuple-element.57), channel_id=1, source_target_pairs={{0,8},{8,0},{16,24},{24,16},{1,9},{9,1},{17,25},{25,17},{2,10},{10... | collective-permute-start | bytes 393224 | tf_op jit(solution)/shard_map/ppermute | solution.py:303
  43.9 7.9 %collective-permute-start.19 = (bf16[256,256]{1,0:T(8,128)(2,1)S(1)}, bf16[256,256]{1,0:T(8,128)(2,1)S(1)}, u32[]{:S(2)}, u32[]{:S(2)}) collective-permute-start(bf16[256,256]{1,0:T(8,128)(2,1)S(1)} %get-tuple-element.58), channel_id=1, source_target_pairs={{0,16},{8,24},{16,0},{24,8},{1,17},{9,25},{17,1},{25,9},{2,18},{10... | collective-permute-start | bytes 393224 | tf_op jit(solution)/shard_map/ppermute | solution.py:303
  45.4 6.4 %collective-permute-start.20 = (bf16[256,256]{1,0:T(8,128)(2,1)S(1)}, bf16[256,256]{1,0:T(8,128)(2,1)S(1)}, u32[]{:S(2)}, u32[]{:S(2)}) collective-permute-start(bf16[256,256]{1,0:T(8,128)(2,1)S(1)} %get-tuple-element.59), channel_id=1, source_target_pairs={{0,24},{8,16},{16,8},{24,0},{1,25},{9,17},{17,9},{25,1},{2,26},{10... | collective-permute-start | bytes 393224 | tf_op jit(solution)/shard_map/ppermute | solution.py:303
  45.4 5.0 %collective-permute-start.8 = (bf16[256,128]{1,0:T(8,128)(2,1)S(1)}, bf16[256,128]{1,0:T(8,128)(2,1)S(1)}, u32[]{:S(2)}, u32[]{:S(2)}) collective-permute-start(bf16[256,128]{1,0:T(8,128)(2,1)S(1)} %get-tuple-element.45), channel_id=1, source_target_pairs={{0,2},{1,3},{2,0},{3,1},{4,6},{5,7},{6,4},{7,5},{8,10},{9,11},{10,... | collective-permute-start | bytes 196616 | tf_op jit(solution)/shard_map/ppermute | solution.py:303
  46.0 5.8 %collective-permute-start.9 = (bf16[256,128]{1,0:T(8,128)(2,1)S(1)}, bf16[256,128]{1,0:T(8,128)(2,1)S(1)}, u32[]{:S(2)}, u32[]{:S(2)}) collective-permute-start(bf16[256,128]{1,0:T(8,128)(2,1)S(1)} %get-tuple-element.46), channel_id=1, source_target_pairs={{0,3},{1,2},{2,1},{3,0},{4,7},{5,6},{6,5},{7,4},{8,11},{9,10},{10,... | collective-permute-start | bytes 196616 | tf_op jit(solution)/shard_map/ppermute | solution.py:303

commit v2 on v1

--- a/solution.py
+++ b/solution.py
@@ -34,7 +34,7 @@
     return pl.ds(pl.multiple_of((lax.axis_index(axis) ^ k) * rows, rows), rows)
 
 
-def call(kernel, out_specs, out_shape, scratch, flops, moved, mib, operands, in_specs=None):
+def call(kernel, out_specs, out_shape, scratch, flops, moved, mib, operands, in_specs=None, aliases={}):
     vmem = pl.BlockSpec(memory_space=pltpu.VMEM)
     return list(pl.pallas_call(
         kernel,
@@ -42,6 +42,7 @@
         out_specs=out_specs or [vmem] * len(out_shape),
         out_shape=out_shape,
         scratch_shapes=scratch,
+        input_output_aliases=aliases,
         compiler_params=pltpu.CompilerParams(vmem_limit_bytes=mib * 2**20),
         cost_estimate=pl.CostEstimate(flops=flops, bytes_accessed=moved, transcendentals=0),
     )(*operands))
@@ -252,11 +253,12 @@
     )
 
 
-def finish_kernel(axis, shares, scale, base_ref, pr_ref, vb_ref, *refs):
-    count = len(refs) - shares - 7
-    back_refs, term_refs = refs[:count], refs[count : count + shares]
-    pre_out, value_out, grad_out, pre_buf, value_buf, grad_buf, sems = refs[count + shares :]
-    rows = back_refs[0].shape[0]
+def finish_kernel(axis, ks, held, scale, base_ref, pr_ref, vb_ref, *refs):
+    refs = refs[held:]
+    back_refs, refs = refs[: len(ks)], refs[len(ks) :]
+    term_refs, refs = (refs[:-7], refs[-7:]) if held else ((), refs)
+    pre_out, value_out, *grad, pre_buf, value_buf, sems = refs
+    rows = pre_buf.shape[1]
     copies = []
 
     def send(source, target, sem):
@@ -264,38 +266,42 @@
         copy.start()
         copies.append(copy)
 
-    for k, back_ref in enumerate(back_refs):
+    for i, (k, back_ref) in enumerate(zip(ks, back_refs)):
         block = peer_rows(axis, k, rows)
         summed = back_ref[...].astype(f32) + base_ref[block]
-        pre_buf[k] = (summed * vb_ref[block].astype(f32)).astype(bf16)
-        value_buf[k] = (summed * pr_ref[block].astype(f32)).astype(bf16)
-        send(pre_buf.at[k], pre_out.at[block], sems.at[0, k])
-        send(value_buf.at[k], value_out.at[block], sems.at[1, k])
-    grad_buf[...] = sum(term_ref[...].astype(f32) for term_ref in term_refs) * scale
-    send(grad_buf, grad_out, sems.at[2, 0])
+        pre_buf[i] = (summed * vb_ref[block].astype(f32)).astype(bf16)
+        value_buf[i] = (summed * pr_ref[block].astype(f32)).astype(bf16)
+        send(pre_buf.at[i], pre_out.at[block], sems.at[0, i])
+        send(value_buf.at[i], value_out.at[block], sems.at[1, i])
+    if held:
+        grad_out, grad_buf = grad
+        grad_buf[...] = sum(term_ref[...].astype(f32) for term_ref in term_refs) * scale
+        send(grad_buf, grad_out, sems.at[2, 0])
     for copy in copies:
         copy.wait()
 
 
-def finish(back, base, pre_gate, value_branch, terms, scale, axis):
-    count = len(back)
+def finish(back, ks, base, pre_gate, value_branch, axis, held=(), terms=(), scale=1.0):
     rows, block = back[0].shape
-    channels = count * rows
+    channels = pre_gate.shape[0]
+    vmem = pl.BlockSpec(memory_space=pltpu.VMEM)
+    hbm = pl.BlockSpec(memory_space=pltpu.HBM)
+    out_shape = [jax.ShapeDtypeStruct((channels, block), bf16)] * 2
+    buffers = [pltpu.VMEM((len(ks), rows, block), bf16)] * 2
+    if held:
+        out_shape.append(jax.ShapeDtypeStruct(terms[0].shape, f32))
+        buffers.insert(0, pltpu.VMEM(terms[0].shape, f32))
     return call(
-        functools.partial(finish_kernel, axis, len(terms), scale),
-        [pl.BlockSpec(memory_space=pltpu.HBM)] * 3,
-        [jax.ShapeDtypeStruct((channels, block), bf16)] * 2
-        + [jax.ShapeDtypeStruct(terms[0].shape, f32)],
-        [
-            pltpu.VMEM((count, rows, block), bf16),
-            pltpu.VMEM((count, rows, block), bf16),
-            pltpu.VMEM(terms[0].shape, f32),
-            pltpu.SemaphoreType.DMA((3, count)),
-        ],
-        3 * channels * block,
-        14 * channels * block,
+        functools.partial(finish_kernel, axis, ks, len(held), scale),
+        [hbm] * len(out_shape),
+        out_shape,
+        buffers + [pltpu.SemaphoreType.DMA((3, len(ks)))],
+        3 * len(ks) * rows * block,
+        14 * len(ks) * rows * block,
         8,
-        (base, pre_gate, value_branch, *back, *terms),
+        (base, pre_gate, value_branch, *held, *back, *terms),
+        [vmem] * 3 + [hbm] * len(held) + [vmem] * (len(back) + len(terms)),
+        {3 + i: i for i in range(len(held))},
     )
 
 
@@ -331,8 +337,11 @@
     back = corr[:1] + [swap(corr[k], "ctx", k) for k in range(1, groups)]
     terms = gradient_dense(both + saved, w, grad_spec, "ctx", "dp")
     terms = terms[:1] + [swap(terms[k], "dp", k) for k in range(1, shares)]
+    early = near[:1] + far
+    held = finish([back[k] for k in early], early, base, rows[2], rows[3], "ctx")
     grad_pre_gate, grad_value_branch, grad_long_filter = finish(
-        back, base, rows[2], rows[3], terms, 1.0 / math.sqrt(token_count), "ctx"
+        [back[k] for k in near[1:]], near[1:], base, rows[2], rows[3], "ctx",
+        held, terms, 1.0 / math.sqrt(token_count),
     )
     shape = grad_output.shape
     return (grad_pre_gate.reshape(shape), grad_value_branch.reshape(shape), grad_long_filter)

time: 53.3 us -> 53 us (level)
  waiting for transfers between devices: 9.65 us -> 8.24 us
  Pallas kernels: 10.6 us -> 11.3 us
    ppermute x21, waiting for transfers between devices: 9.65 us -> 8.24 us  [swap(): lax.ppermute(value, axis, [(j, j ^ k) for j in range(lax.axis_size(axis))])]
    pallas_call x6 -> x7, Pallas kernels: 10.6 us -> 11.3 us  [call(): pl.pallas_call(kernel, in_specs=in_specs or [vmem] * len(operands), out_s...]
  transfers between devices with their start and end apart: 21 -> 21, of which waited for: 5 -> 5; matrix products, arithmetic and copies ran while one was open for 1% -> 1% of each run, Pallas kernels for 15% -> 17%
where the time goes in v2:
time: 53 us; the launch traced here: 52.8 us
  starting transfers between devices  32.2 us (61%)
  Pallas kernels  11.3 us (21%)
  waiting for transfers between devices  8.24 us (16%)
  between operations  0.78 us (1%)
    ppermute x21, starting transfers between devices, swap(): lax.ppermute(value, axis, [(j, j ^ k) for j in range(lax.axis_size(axis))])  32.2 us
    pallas_call x7, Pallas kernels, call(): pl.pallas_call(kernel, in_specs=in_specs or [vmem] * len(operands), out_s...  11.3 us
    ppermute x21, waiting for transfers between devices, swap(): lax.ppermute(value, axis, [(j, j ^ k) for j in range(lax.axis_size(axis))])  8.24 us
  transfers between devices with their start and end apart: 21, of which 5 were waited for; matrix products, arithmetic and copies ran while one was open for 1% of the time, Pallas kernels for 17%

profile of v2, /device:TPU:0, one launch (start us, length us, event | category | flops | bytes accessed | tf_op | source)
XLA Modules:
  0.0 52.8 jit_solution(18227381337778827112)
XLA Ops:
  0.6 0.0 copy-start.3
  0.7 1.3 %shard_map.96 = (bf16[256,128]{1,0:T(8,128)(2,1)S(1)}, bf16[256,128]{1,0:T(8,128)(2,1)S(1)}, bf16[256,128]{1,0:T(8,128)(2,1)S(1)}, bf16[256,128]{1,0:T(8,128)(2,1)S(1)}) custom-call(bf16[2048,128]{1,0:T(8,128)(2,1)} %bitcast.16, bf16[2048,128]{1,0:T(8,128)(2,1)} %bitcast.14), custom_call_target="tpu_custom_call" | custom-call | flops 131072 | bytes 786432 | tf_op jit(solution)/shard_map/pallas_call | solution.py:39
  2.0 4.1 %collective-permute-start.3 = (bf16[256,128]{1,0:T(8,128)(2,1)S(1)}, bf16[256,128]{1,0:T(8,128)(2,1)S(1)}, u32[]{:S(2)}, u32[]{:S(2)}) collective-permute-start(bf16[256,128]{1,0:T(8,128)(2,1)S(1)} %get-tuple-element.41), channel_id=1, source_target_pairs={{0,4},{1,5},{2,6},{3,7},{4,0},{5,1},{6,2},{7,3},{8,12},{9,13},{10,... | collective-permute-start | bytes 196616 | tf_op jit(solution)/shard_map/ppermute | solution.py:309
  6.1 1.3 %collective-permute-start.4 = (bf16[256,128]{1,0:T(8,128)(2,1)S(1)}, bf16[256,128]{1,0:T(8,128)(2,1)S(1)}, u32[]{:S(2)}, u32[]{:S(2)}) collective-permute-start(bf16[256,128]{1,0:T(8,128)(2,1)S(1)} %get-tuple-element.42), channel_id=1, source_target_pairs={{0,5},{1,4},{2,7},{3,6},{4,1},{5,0},{6,3},{7,2},{8,13},{9,12},{10,... | collective-permute-start | bytes 196616 | tf_op jit(solution)/shard_map/ppermute | solution.py:309
  7.4 1.6 %shard_map.95 = (bf16[2,256,128]{2,1,0:T(8,128)(2,1)S(1)}, bf16[2,256,128]{2,1,0:T(8,128)(2,1)S(1)}, bf16[2,256,128]{2,1,0:T(8,128)(2,1)S(1)}, bf16[2,256,128]{2...) custom-call(bf16[2048,128]{1,0:T(8,128)(2,1)} %bitcast.17, ...), custom_call_target="tpu_custom_call" | custom-call | flops 393216 | bytes 2359296 | tf_op jit(solution)/shard_map/pallas_call | solution.py:39
  9.0 0.3 collective-permute-start
  9.3 1.8 %collective-permute-start.1 = (bf16[2,256,128]{2,1,0:T(8,128)(2,1)S(1)}, bf16[2,256,128]{2,1,0:T(8,128)(2,1)S(1)}, u32[]{:S(2)}, u32[]{:S(2)}) collective-permute-start(bf16[2,256,128]{2,1,0:T(8,128)(2,1)S(1)} %get-tuple-element.39), channel_id=1, source_target_pairs={{0,2},{1,3},{2,0},{3,1},{4,6},{5,7},{6,4},{7,5},{8,10},{9,11},{10,... | collective-permute-start | bytes 393224 | tf_op jit(solution)/shard_map/ppermute | solution.py:309
  11.2 1.4 %collective-permute-start.2 = (bf16[2,256,128]{2,1,0:T(8,128)(2,1)S(1)}, bf16[2,256,128]{2,1,0:T(8,128)(2,1)S(1)}, u32[]{:S(2)}, u32[]{:S(2)}) collective-permute-start(bf16[2,256,128]{2,1,0:T(8,128)(2,1)S(1)} %get-tuple-element.40), channel_id=1, source_target_pairs={{0,3},{1,2},{2,1},{3,0},{4,7},{5,6},{6,5},{7,4},{8,11},{9,10},{10,... | collective-permute-start | bytes 393224 | tf_op jit(solution)/shard_map/ppermute | solution.py:309
  12.6 0.0 collective-permute-done.3.refs_4_
  12.6 3.6 %collective-permute-start.5 = (bf16[256,128]{1,0:T(8,128)(2,1)S(1)}, bf16[256,128]{1,0:T(8,128)(2,1)S(1)}, u32[]{:S(2)}, u32[]{:S(2)}) collective-permute-start(bf16[256,128]{1,0:T(8,128)(2,1)S(1)} %get-tuple-element.43), channel_id=1, source_target_pairs={{0,6},{1,7},{2,4},{3,5},{4,2},{5,3},{6,0},{7,1},{8,14},{9,15},{10,... | collective-permute-start | bytes 196616 | tf_op jit(solution)/shard_map/ppermute | solution.py:309
  16.2 0.0 collective-permute-done.4.refs_5_
  16.2 0.8 %collective-permute-start.6 = (bf16[256,128]{1,0:T(8,128)(2,1)S(1)}, bf16[256,128]{1,0:T(8,128)(2,1)S(1)}, u32[]{:S(2)}, u32[]{:S(2)}) collective-permute-start(bf16[256,128]{1,0:T(8,128)(2,1)S(1)} %get-tuple-element.44), channel_id=1, source_target_pairs={{0,7},{1,6},{2,5},{3,4},{4,3},{5,2},{6,1},{7,0},{8,15},{9,14},{10,... | collective-permute-start | bytes 196616 | tf_op jit(solution)/shard_map/ppermute | solution.py:309
  17.0 1.4 %shard_map.94 = (bf16[512,2048]{1,0:T(8,128)(2,1)S(1)}, f32[256,2048]{1,0:T(8,128)S(1)}) custom-call(f32[256,1024]{1,0:T(8,128)S(1)} %copy-done.2, bf16[512,2048]{1,0:T(8,128)(2,1)S(1)} %copy-done.3), custom_call_target="tpu_custom_call" | custom-call | flops 1073741824 | bytes 7340032 | tf_op jit(solution)/shard_map/pallas_call | solution.py:39
  18.4 3.5 %collective-permute-done.5.refs_6_ = bf16[256,128]{1,0:T(8,128)(2,1)S(1)} collective-permute-done((bf16[256,128]{1,0:T(8,128)(2,1)S(1)}, bf16[256,128]{1,0:T(8,128)(2,1)S(1)}, u32[]{:S(2)}, u32[]{:S(2)}) %collective-permute-start.5) | collective-permute-done | bytes 65568 | tf_op jit(solution)/shard_map/ppermute | solution.py:309
  21.9 0.0 collective-permute-start.14
  21.9 1.6 %collective-permute-done.6.refs_7_ = bf16[256,128]{1,0:T(8,128)(2,1)S(1)} collective-permute-done((bf16[256,128]{1,0:T(8,128)(2,1)S(1)}, bf16[256,128]{1,0:T(8,128)(2,1)S(1)}, u32[]{:S(2)}, u32[]{:S(2)}) %collective-permute-start.6) | collective-permute-done | bytes 65568 | tf_op jit(solution)/shard_map/ppermute | solution.py:309
  23.5 1.3 %collective-permute-start.15 = (bf16[256,128]{1,0:T(8,128)(2,1)S(1)}, bf16[256,128]{1,0:T(8,128)(2,1)S(1)}, u32[]{:S(2)}, u32[]{:S(2)}) collective-permute-start(bf16[256,128]{1,0:T(8,128)(2,1)S(1)} %get-tuple-element.57), channel_id=1, source_target_pairs={{0,5},{1,4},{2,7},{3,6},{4,1},{5,0},{6,3},{7,2},{8,13},{9,12},{10,... | collective-permute-start | bytes 196616 | tf_op jit(solution)/shard_map/ppermute | solution.py:309
  24.8 0.0 collective-permute-done.refs_1_
  24.8 1.1 %collective-permute-start.16 = (bf16[256,128]{1,0:T(8,128)(2,1)S(1)}, bf16[256,128]{1,0:T(8,128)(2,1)S(1)}, u32[]{:S(2)}, u32[]{:S(2)}) collective-permute-start(bf16[256,128]{1,0:T(8,128)(2,1)S(1)} %get-tuple-element.58), channel_id=1, source_target_pairs={{0,6},{1,7},{2,4},{3,5},{4,2},{5,3},{6,0},{7,1},{8,14},{9,15},{10,... | collective-permute-start | bytes 196616 | tf_op jit(solution)/shard_map/ppermute | solution.py:309
  25.9 0.0 collective-permute-done.1.refs_2_
  25.9 3.6 %collective-permute-start.17 = (bf16[256,128]{1,0:T(8,128)(2,1)S(1)}, bf16[256,128]{1,0:T(8,128)(2,1)S(1)}, u32[]{:S(2)}, u32[]{:S(2)}) collective-permute-start(bf16[256,128]{1,0:T(8,128)(2,1)S(1)} %get-tuple-element.59), channel_id=1, source_target_pairs={{0,7},{1,6},{2,5},{3,4},{4,3},{5,2},{6,1},{7,0},{8,15},{9,14},{10,... | collective-permute-start | bytes 196616 | tf_op jit(solution)/shard_map/ppermute | solution.py:309
  29.5 0.0 collective-permute-done.2.refs_3_
  29.5 2.5 %shard_map.97 = (bf16[256,128]{1,0:T(8,128)(2,1)S(1)}, bf16[256,128]{1,0:T(8,128)(2,1)S(1)}, bf16[256,128]{1,0:T(8,128)(2,1)S(1)}, bf16[256,128]{1,0:T(8,128)(2,...) custom-call(bf16[512,2048]{1,0:T(8,128)(2,1)S(1)} %copy-done.3, ...), custom_call_target="tpu_custom_call" | custom-call | flops 2147483648 | bytes 9437184 | tf_op jit(solution)/shard_map/pallas_call | solution.py:39
  32.0 1.2 %collective-permute-start.10 = (bf16[256,128]{1,0:T(8,128)(2,1)S(1)}, bf16[256,128]{1,0:T(8,128)(2,1)S(1)}, u32[]{:S(2)}, u32[]{:S(2)}) collective-permute-start(bf16[256,128]{1,0:T(8,128)(2,1)S(1)} %get-tuple-element.49), channel_id=1, source_target_pairs={{0,7},{1,6},{2,5},{3,4},{4,3},{5,2},{6,1},{7,0},{8,15},{9,14},{10,... | collective-permute-start | bytes 196616 | tf_op jit(solution)/shard_map/ppermute | solution.py:309
  33.2 0.0 collective-permute-done.14.refs_4_
  33.2 3.3 %collective-permute-start.8 = (bf16[256,128]{1,0:T(8,128)(2,1)S(1)}, bf16[256,128]{1,0:T(8,128)(2,1)S(1)}, u32[]{:S(2)}, u32[]{:S(2)}) collective-permute-start(bf16[256,128]{1,0:T(8,128)(2,1)S(1)} %get-tuple-element.47), channel_id=1, source_target_pairs={{0,5},{1,4},{2,7},{3,6},{4,1},{5,0},{6,3},{7,2},{8,13},{9,12},{10,... | collective-permute-start | bytes 196616 | tf_op jit(solution)/shard_map/ppermute | solution.py:309
  36.6 0.0 collective-permute-done.16.refs_6_
  36.6 3.2 %collective-permute-start.9 = (bf16[256,128]{1,0:T(8,128)(2,1)S(1)}, bf16[256,128]{1,0:T(8,128)(2,1)S(1)}, u32[]{:S(2)}, u32[]{:S(2)}) collective-permute-start(bf16[256,128]{1,0:T(8,128)(2,1)S(1)} %get-tuple-element.48), channel_id=1, source_target_pairs={{0,6},{1,7},{2,4},{3,5},{4,2},{5,3},{6,0},{7,1},{8,14},{9,15},{10,... | collective-permute-start | bytes 196616 | tf_op jit(solution)/shard_map/ppermute | solution.py:309
  39.8 0.6 %collective-permute-start.11 = (bf16[256,128]{1,0:T(8,128)(2,1)S(1)}, bf16[256,128]{1,0:T(8,128)(2,1)S(1)}, u32[]{:S(2)}, u32[]{:S(2)}) collective-permute-start(bf16[256,128]{1,0:T(8,128)(2,1)S(1)} %get-tuple-element.52), channel_id=1, source_target_pairs={{0,1},{1,0},{2,3},{3,2},{4,5},{5,4},{6,7},{7,6},{8,9},{9,8},{10,11... | collective-permute-start | bytes 196616 | tf_op jit(solution)/shard_map/ppermute | solution.py:309
  40.3 2.5 %shard_map.99 = (bf16[256,256]{1,0:T(8,128)(2,1)S(1)}, bf16[256,256]{1,0:T(8,128)(2,1)S(1)}, bf16[256,256]{1,0:T(8,128)(2,1)S(1)}, bf16[256,256]{1,0:T(8,128)(2,1)S(1)}) custom-call(bf16[512,2048]{1,0:T(8,128)(2,1)S(1)} %copy-done.3, bf16[512,2048]{1,0:T(8,128)(2,1)S(1)} %get-tuple-element.35.high_ref, f32[256,2048]{1,0:T(8,128)S(1)} %get-tuple-element.55.grad_spec_ref, ...), custom_call_target="tpu_custom_call" | custom-call | flops 2147483648 | bytes 9437184 | tf_op jit(solution)/shard_map/pallas_call | solution.py:39
  42.9 0.0 copy-start
  42.9 0.0 copy-start.1
  42.9 0.0 collective-permute-done.10.refs_4_
  42.9 0.1 collective-permute-start.18
  43.0 0.3 collective-permute-done.7.refs_1_
  43.3 1.5 %collective-permute-start.19 = (bf16[256,256]{1,0:T(8,128)(2,1)S(1)}, bf16[256,256]{1,0:T(8,128)(2,1)S(1)}, u32[]{:S(2)}, u32[]{:S(2)}) collective-permute-start(bf16[256,256]{1,0:T(8,128)(2,1)S(1)} %get-tuple-element.62), channel_id=1, source_target_pairs={{0,16},{8,24},{16,0},{24,8},{1,17},{9,25},{17,1},{25,9},{2,18},{10... | collective-permute-start | bytes 393224 | tf_op jit(solution)/shard_map/ppermute | solution.py:309
  44.8 0.0 collective-permute-start.20
  44.8 0.0 collective-permute-done.9.refs_3_
  44.8 0.8 %collective-permute-start.12 = (bf16[256,128]{1,0:T(8,128)(2,1)S(1)}, bf16[256,128]{1,0:T(8,128)(2,1)S(1)}, u32[]{:S(2)}, u32[]{:S(2)}) collective-permute-start(bf16[256,128]{1,0:T(8,128)(2,1)S(1)} %get-tuple-element.53), channel_id=1, source_target_pairs={{0,2},{1,3},{2,0},{3,1},{4,6},{5,7},{6,4},{7,5},{8,10},{9,11},{10,... | collective-permute-start | bytes 196616 | tf_op jit(solution)/shard_map/ppermute | solution.py:309
  45.7 0.0 collective-permute-done.11.refs_2_
  45.7 2.1 %collective-permute-start.13 = (bf16[256,128]{1,0:T(8,128)(2,1)S(1)}, bf16[256,128]{1,0:T(8,128)(2,1)S(1)}, u32[]{:S(2)}, u32[]{:S(2)}) collective-permute-start(bf16[256,128]{1,0:T(8,128)(2,1)S(1)} %get-tuple-element.54), channel_id=1, source_target_pairs={{0,3},{1,2},{2,1},{3,0},{4,7},{5,6},{6,5},{7,4},{8,11},{9,10},{10,... | collective-permute-start | bytes 196616 | tf_op jit(solution)/shard_map/ppermute | solution.py:309
  47.8 0.3 convert_multiply_fusion.base_ref
  48.1 1.0 %shard_map.98 = (bf16[2048,128]{1,0:T(8,128)(2,1)}, bf16[2048,128]{1,0:T(8,128)(2,1)}) custom-call(f32[2048,128]{1,0:T(8,128)S(1)} %convert_multiply_fusion.base_ref, bf16[2048,128]{1,0:T(8,128)(2,1)S(1)} %bitcast.9, bf16[2048,128]{1,0:T(8,128)(2,1)S(1)} %bitcast.12, bf16[256,128]{1,0:T(8,128)(2,1)S(1)} %get-tuple-element.45.refs_0_, ...), custom_call_target="tpu_custom_call" | custom-call | flops 491520 | bytes 2293760 | tf_op jit(solution)/shard_map/pallas_call | solution.py:39
  49.1 0.3 collective-permute-done.12.refs_3_
  49.4 2.5 %collective-permute-done.13.refs_4_ = bf16[256,128]{1,0:T(8,128)(2,1)S(1)} collective-permute-done((bf16[256,128]{1,0:T(8,128)(2,1)S(1)}, bf16[256,128]{1,0:T(8,128)(2,1)S(1)}, u32[]{:S(2)}, u32[]{:S(2)}) %collective-permute-start.13) | collective-permute-done | bytes 65568 | tf_op jit(solution)/shard_map/ppermute | solution.py:309
  51.9 0.0 collective-permute-done.19.refs_7_
  51.9 0.0 collective-permute-done.20.refs_8_
  51.9 1.0 %shard_map.100 = (bf16[2048,128]{1,0:T(8,128)(2,1)}, bf16[2048,128]{1,0:T(8,128)(2,1)}, f32[256,256]{1,0:T(8,128)}) custom-call(f32[2048,128]{1,0:T(8,128)S(1)} %convert_multiply_fusion.base_ref, bf16[2048,128]{1,0:T(8,128)(2,1)S(1)} %bitcast.10, bf16[2048,128]{1,0:T(8,128)(2,1)S(1)} %bitcast.13, ...), custom_call_target="tpu_custom_call", output_to_operand_aliasing={{0}: (3, {}), {1}: (4, {})} | custom-call | flops 294912 | bytes 1376256 | tf_op jit(solution)/shard_map/pallas_call | solution.py:39
  (16 shorter events, 0.0 us)
Async XLA Ops:
  0.6 16.3 %copy-start.3 = (bf16[512,2048]{1,0:T(8,128)(2,1)S(1)}, bf16[512,2048]{1,0:T(8,128)(2,1)}, u32[]{:S(2)}) copy-start(bf16[512,2048]{1,0:T(8,128)(2,1)} %constant.2.clone.low_ref) | copy-start | bytes 6291460
  0.6 16.3 %copy-start.2 = (f32[256,1024]{1,0:T(8,128)S(1)}, f32[256,1024]{1,0:T(8,128)}, u32[]{:S(2)}) copy-start(f32[256,1024]{1,0:T(8,128)} %filt_ref.1) | copy-start | bytes 3145732
  2.0 10.6 %collective-permute-start.3 = (bf16[256,128]{1,0:T(8,128)(2,1)S(1)}, bf16[256,128]{1,0:T(8,128)(2,1)S(1)}, u32[]{:S(2)}, u32[]{:S(2)}) collective-permute-start(bf16[256,128]{1,0:T(8,128)(2,1)S(1)} %get-tuple-element.41), channel_id=1, source_target_pairs={{0,4},{1,5},{2,6},{3,7},{4,0},{5,1},{6,2},{7,3},{8,12},{9,13},{10,... | collective-permute-start | bytes 196616 | tf_op jit(solution)/shard_map/ppermute | solution.py:309
  6.1 10.1 %collective-permute-start.4 = (bf16[256,128]{1,0:T(8,128)(2,1)S(1)}, bf16[256,128]{1,0:T(8,128)(2,1)S(1)}, u32[]{:S(2)}, u32[]{:S(2)}) collective-permute-start(bf16[256,128]{1,0:T(8,128)(2,1)S(1)} %get-tuple-element.42), channel_id=1, source_target_pairs={{0,5},{1,4},{2,7},{3,6},{4,1},{5,0},{6,3},{7,2},{8,13},{9,12},{10,... | collective-permute-start | bytes 196616 | tf_op jit(solution)/shard_map/ppermute | solution.py:309
  9.0 15.8 %collective-permute-start = (bf16[2,256,128]{2,1,0:T(8,128)(2,1)S(1)}, bf16[2,256,128]{2,1,0:T(8,128)(2,1)S(1)}, u32[]{:S(2)}, u32[]{:S(2)}) collective-permute-start(bf16[2,256,128]{2,1,0:T(8,128)(2,1)S(1)} %get-tuple-element.38), channel_id=1, source_target_pairs={{0,1},{1,0},{2,3},{3,2},{4,5},{5,4},{6,7},{7,6},{8,9},{9,8},{10,11... | collective-permute-start | bytes 393224 | tf_op jit(solution)/shard_map/ppermute | solution.py:309
  9.3 16.6 %collective-permute-start.1 = (bf16[2,256,128]{2,1,0:T(8,128)(2,1)S(1)}, bf16[2,256,128]{2,1,0:T(8,128)(2,1)S(1)}, u32[]{:S(2)}, u32[]{:S(2)}) collective-permute-start(bf16[2,256,128]{2,1,0:T(8,128)(2,1)S(1)} %get-tuple-element.39), channel_id=1, source_target_pairs={{0,2},{1,3},{2,0},{3,1},{4,6},{5,7},{6,4},{7,5},{8,10},{9,11},{10,... | collective-permute-start | bytes 393224 | tf_op jit(solution)/shard_map/ppermute | solution.py:309
  11.2 18.4 %collective-permute-start.2 = (bf16[2,256,128]{2,1,0:T(8,128)(2,1)S(1)}, bf16[2,256,128]{2,1,0:T(8,128)(2,1)S(1)}, u32[]{:S(2)}, u32[]{:S(2)}) collective-permute-start(bf16[2,256,128]{2,1,0:T(8,128)(2,1)S(1)} %get-tuple-element.40), channel_id=1, source_target_pairs={{0,3},{1,2},{2,1},{3,0},{4,7},{5,6},{6,5},{7,4},{8,11},{9,10},{10,... | collective-permute-start | bytes 393224 | tf_op jit(solution)/shard_map/ppermute | solution.py:309
  12.6 9.3 %collective-permute-start.5 = (bf16[256,128]{1,0:T(8,128)(2,1)S(1)}, bf16[256,128]{1,0:T(8,128)(2,1)S(1)}, u32[]{:S(2)}, u32[]{:S(2)}) collective-permute-start(bf16[256,128]{1,0:T(8,128)(2,1)S(1)} %get-tuple-element.43), channel_id=1, source_target_pairs={{0,6},{1,7},{2,4},{3,5},{4,2},{5,3},{6,0},{7,1},{8,14},{9,15},{10,... | collective-permute-start | bytes 196616 | tf_op jit(solution)/shard_map/ppermute | solution.py:309
  16.2 7.3 %collective-permute-start.6 = (bf16[256,128]{1,0:T(8,128)(2,1)S(1)}, bf16[256,128]{1,0:T(8,128)(2,1)S(1)}, u32[]{:S(2)}, u32[]{:S(2)}) collective-permute-start(bf16[256,128]{1,0:T(8,128)(2,1)S(1)} %get-tuple-element.44), channel_id=1, source_target_pairs={{0,7},{1,6},{2,5},{3,4},{4,3},{5,2},{6,1},{7,0},{8,15},{9,14},{10,... | collective-permute-start | bytes 196616 | tf_op jit(solution)/shard_map/ppermute | solution.py:309
  21.9 11.4 %collective-permute-start.14 = (bf16[256,128]{1,0:T(8,128)(2,1)S(1)}, bf16[256,128]{1,0:T(8,128)(2,1)S(1)}, u32[]{:S(2)}, u32[]{:S(2)}) collective-permute-start(bf16[256,128]{1,0:T(8,128)(2,1)S(1)} %get-tuple-element.56), channel_id=1, source_target_pairs={{0,4},{1,5},{2,6},{3,7},{4,0},{5,1},{6,2},{7,3},{8,12},{9,13},{10,... | collective-permute-start | bytes 196616 | tf_op jit(solution)/shard_map/ppermute | solution.py:309
  23.5 9.8 %collective-permute-start.15 = (bf16[256,128]{1,0:T(8,128)(2,1)S(1)}, bf16[256,128]{1,0:T(8,128)(2,1)S(1)}, u32[]{:S(2)}, u32[]{:S(2)}) collective-permute-start(bf16[256,128]{1,0:T(8,128)(2,1)S(1)} %get-tuple-element.57), channel_id=1, source_target_pairs={{0,5},{1,4},{2,7},{3,6},{4,1},{5,0},{6,3},{7,2},{8,13},{9,12},{10,... | collective-permute-start | bytes 196616 | tf_op jit(solution)/shard_map/ppermute | solution.py:309
  24.8 11.8 %collective-permute-start.16 = (bf16[256,128]{1,0:T(8,128)(2,1)S(1)}, bf16[256,128]{1,0:T(8,128)(2,1)S(1)}, u32[]{:S(2)}, u32[]{:S(2)}) collective-permute-start(bf16[256,128]{1,0:T(8,128)(2,1)S(1)} %get-tuple-element.58), channel_id=1, source_target_pairs={{0,6},{1,7},{2,4},{3,5},{4,2},{5,3},{6,0},{7,1},{8,14},{9,15},{10,... | collective-permute-start | bytes 196616 | tf_op jit(solution)/shard_map/ppermute | solution.py:309
  25.9 13.8 %collective-permute-start.17 = (bf16[256,128]{1,0:T(8,128)(2,1)S(1)}, bf16[256,128]{1,0:T(8,128)(2,1)S(1)}, u32[]{:S(2)}, u32[]{:S(2)}) collective-permute-start(bf16[256,128]{1,0:T(8,128)(2,1)S(1)} %get-tuple-element.59), channel_id=1, source_target_pairs={{0,7},{1,6},{2,5},{3,4},{4,3},{5,2},{6,1},{7,0},{8,15},{9,14},{10,... | collective-permute-start | bytes 196616 | tf_op jit(solution)/shard_map/ppermute | solution.py:309
  32.0 10.9 %collective-permute-start.10 = (bf16[256,128]{1,0:T(8,128)(2,1)S(1)}, bf16[256,128]{1,0:T(8,128)(2,1)S(1)}, u32[]{:S(2)}, u32[]{:S(2)}) collective-permute-start(bf16[256,128]{1,0:T(8,128)(2,1)S(1)} %get-tuple-element.49), channel_id=1, source_target_pairs={{0,7},{1,6},{2,5},{3,4},{4,3},{5,2},{6,1},{7,0},{8,15},{9,14},{10,... | collective-permute-start | bytes 196616 | tf_op jit(solution)/shard_map/ppermute | solution.py:309
  33.2 10.1 %collective-permute-start.7 = (bf16[256,128]{1,0:T(8,128)(2,1)S(1)}, bf16[256,128]{1,0:T(8,128)(2,1)S(1)}, u32[]{:S(2)}, u32[]{:S(2)}) collective-permute-start(bf16[256,128]{1,0:T(8,128)(2,1)S(1)} %get-tuple-element.46), channel_id=1, source_target_pairs={{0,4},{1,5},{2,6},{3,7},{4,0},{5,1},{6,2},{7,3},{8,12},{9,13},{10,... | collective-permute-start | bytes 196616 | tf_op jit(solution)/shard_map/ppermute | solution.py:309
  33.2 11.6 %collective-permute-start.8 = (bf16[256,128]{1,0:T(8,128)(2,1)S(1)}, bf16[256,128]{1,0:T(8,128)(2,1)S(1)}, u32[]{:S(2)}, u32[]{:S(2)}) collective-permute-start(bf16[256,128]{1,0:T(8,128)(2,1)S(1)} %get-tuple-element.47), channel_id=1, source_target_pairs={{0,5},{1,4},{2,7},{3,6},{4,1},{5,0},{6,3},{7,2},{8,13},{9,12},{10,... | collective-permute-start | bytes 196616 | tf_op jit(solution)/shard_map/ppermute | solution.py:309
  36.6 8.3 %collective-permute-start.9 = (bf16[256,128]{1,0:T(8,128)(2,1)S(1)}, bf16[256,128]{1,0:T(8,128)(2,1)S(1)}, u32[]{:S(2)}, u32[]{:S(2)}) collective-permute-start(bf16[256,128]{1,0:T(8,128)(2,1)S(1)} %get-tuple-element.48), channel_id=1, source_target_pairs={{0,6},{1,7},{2,4},{3,5},{4,2},{5,3},{6,0},{7,1},{8,14},{9,15},{10,... | collective-permute-start | bytes 196616 | tf_op jit(solution)/shard_map/ppermute | solution.py:309
  39.8 5.9 %collective-permute-start.11 = (bf16[256,128]{1,0:T(8,128)(2,1)S(1)}, bf16[256,128]{1,0:T(8,128)(2,1)S(1)}, u32[]{:S(2)}, u32[]{:S(2)}) collective-permute-start(bf16[256,128]{1,0:T(8,128)(2,1)S(1)} %get-tuple-element.52), channel_id=1, source_target_pairs={{0,1},{1,0},{2,3},{3,2},{4,5},{5,4},{6,7},{7,6},{8,9},{9,8},{10,11... | collective-permute-start | bytes 196616 | tf_op jit(solution)/shard_map/ppermute | solution.py:309
  40.3 7.4 %copy-start.4 = (bf16[1,2048,128]{2,1,0:T(8,128)(2,1)S(1)}, bf16[1,2048,128]{2,1,0:T(8,128)(2,1)}, u32[]{:S(2)}) copy-start(bf16[1,2048,128]{2,1,0:T(8,128)(2,1)} %param.8) | copy-start | bytes 1572868
  40.3 7.4 %copy-start.5 = (bf16[1,2048,128]{2,1,0:T(8,128)(2,1)S(1)}, bf16[1,2048,128]{2,1,0:T(8,128)(2,1)}, u32[]{:S(2)}) copy-start(bf16[1,2048,128]{2,1,0:T(8,128)(2,1)} %param.7) | copy-start | bytes 1572868
  40.3 7.4 %copy-start.6 = (f32[2048]{0:T(1024)S(1)}, f32[2048]{0:T(1024)}, u32[]{:S(2)}) copy-start(f32[2048]{0:T(1024)} %param.12) | copy-start | bytes 24580
  42.9 5.3 %copy-start = (bf16[1,2048,128]{2,1,0:T(8,128)(2,1)S(1)}, bf16[1,2048,128]{2,1,0:T(8,128)(2,1)}, u32[]{:S(2)}) copy-start(bf16[1,2048,128]{2,1,0:T(8,128)(2,1)} %param.9) | copy-start | bytes 1572868
  42.9 5.3 %copy-start.1 = (bf16[1,2048,128]{2,1,0:T(8,128)(2,1)S(1)}, bf16[1,2048,128]{2,1,0:T(8,128)(2,1)}, u32[]{:S(2)}) copy-start(bf16[1,2048,128]{2,1,0:T(8,128)(2,1)} %param.10) | copy-start | bytes 1572868
  42.9 9.0 %collective-permute-start.18 = (bf16[256,256]{1,0:T(8,128)(2,1)S(1)}, bf16[256,256]{1,0:T(8,128)(2,1)S(1)}, u32[]{:S(2)}, u32[]{:S(2)}) collective-permute-start(bf16[256,256]{1,0:T(8,128)(2,1)S(1)} %get-tuple-element.61), channel_id=1, source_target_pairs={{0,8},{8,0},{16,24},{24,16},{1,9},{9,1},{17,25},{25,17},{2,10},{10... | collective-permute-start | bytes 393224 | tf_op jit(solution)/shard_map/ppermute | solution.py:309
  43.3 8.5 %collective-permute-start.19 = (bf16[256,256]{1,0:T(8,128)(2,1)S(1)}, bf16[256,256]{1,0:T(8,128)(2,1)S(1)}, u32[]{:S(2)}, u32[]{:S(2)}) collective-permute-start(bf16[256,256]{1,0:T(8,128)(2,1)S(1)} %get-tuple-element.62), channel_id=1, source_target_pairs={{0,16},{8,24},{16,0},{24,8},{1,17},{9,25},{17,1},{25,9},{2,18},{10... | collective-permute-start | bytes 393224 | tf_op jit(solution)/shard_map/ppermute | solution.py:309
  44.8 7.1 %collective-permute-start.20 = (bf16[256,256]{1,0:T(8,128)(2,1)S(1)}, bf16[256,256]{1,0:T(8,128)(2,1)S(1)}, u32[]{:S(2)}, u32[]{:S(2)}) collective-permute-start(bf16[256,256]{1,0:T(8,128)(2,1)S(1)} %get-tuple-element.63), channel_id=1, source_target_pairs={{0,24},{8,16},{16,8},{24,0},{1,25},{9,17},{17,9},{25,1},{2,26},{10... | collective-permute-start | bytes 393224 | tf_op jit(solution)/shard_map/ppermute | solution.py:309
  44.8 4.5 %collective-permute-start.12 = (bf16[256,128]{1,0:T(8,128)(2,1)S(1)}, bf16[256,128]{1,0:T(8,128)(2,1)S(1)}, u32[]{:S(2)}, u32[]{:S(2)}) collective-permute-start(bf16[256,128]{1,0:T(8,128)(2,1)S(1)} %get-tuple-element.53), channel_id=1, source_target_pairs={{0,2},{1,3},{2,0},{3,1},{4,6},{5,7},{6,4},{7,5},{8,10},{9,11},{10,... | collective-permute-start | bytes 196616 | tf_op jit(solution)/shard_map/ppermute | solution.py:309
  45.7 6.2 %collective-permute-start.13 = (bf16[256,128]{1,0:T(8,128)(2,1)S(1)}, bf16[256,128]{1,0:T(8,128)(2,1)S(1)}, u32[]{:S(2)}, u32[]{:S(2)}) collective-permute-start(bf16[256,128]{1,0:T(8,128)(2,1)S(1)} %get-tuple-element.54), channel_id=1, source_target_pairs={{0,3},{1,2},{2,1},{3,0},{4,7},{5,6},{6,5},{7,4},{8,11},{9,10},{10,... | collective-permute-start | bytes 196616 | tf_op jit(solution)/shard_map/ppermute | solution.py:309
